TPU v7x, 32 devices: a whole 2x2x4 slice. The times are simulated.
32 devices in a mesh: gx: 2 (over x), gy: 4 (over z), wa: 4 (over y, core).
Axes of the slice: x: 2, y: 2, z: 4, core: 2. Of those that a mesh axis runs over, the one named last changes fastest.
Arguments:
- velocity: float32 [3, 64, 256, 512], P(None, 'gx', 'gy', 'wa'), may hold values from -70 to 70, as said below
- lengths: int32 [2, 4, 4, 2048], P('gx', 'gy', 'wa'), may hold values from 16 to 128
- destinations: int32 [2, 4, 4, 2048, 1], P('gx', 'gy', 'wa'), may hold values from 0 to 7; in each aligned block of 2048 rows (0 to 2047, 2048 to 4095, ..., all dimensions but the last counted through in order) at most 512 rows name the same one
Outputs:
- received: float32 [8, 4, 3, 8, 512, 128], P(('gx', 'gy'), 'wa')
Inputs may be any that keep to these rules, and one draw needn't show every extreme that they name: `velocity`: finite values; the amplitude varies over the grid. `destinations`: in every draw no device sends more than 512 blocks to one writer, and some device sends exactly 512 to one writer.
All inputs are finite; a program needn't handle non-finite values.
Results may differ from a plain program's by a relative error of at most 0.0003.
Values sent between devices are 32-bit elements; how exact they have to be, the bound alone decides.
A program may use at most 128 MiB of HBM per device.

v0:
```python
import functools

import jax
import jax.numpy as jnp
import numpy as np
from jax import lax
from jax.experimental import pallas as pl
from jax.experimental.pallas import tpu as pltpu
from jax.sharding import PartitionSpec as P

BY = 8
BZ = 16
UNROLL = 2
MESH = pl.DeviceIdType.MESH


def dct_table(count):
    freqs, points = np.arange(count)[:, None], np.arange(count)[None, :]
    table = np.cos(np.pi * (points + 0.5) * freqs / count) * np.sqrt(2.0 / count)
    return np.where(freqs == 0, table * np.sqrt(0.5), table)


def split_table():
    kron = np.kron(dct_table(BY), dct_table(BZ)).T.astype(np.float32)
    high = kron.astype(jnp.bfloat16)
    low = (kron - high.astype(np.float32)).astype(jnp.bfloat16)
    return np.block([[high, low], [high, np.zeros_like(low)]]).astype(jnp.bfloat16)


def faces_kernel(writers, capacity, targets, vel, slots, y_faces, z_faces):
    comps, cells_x, cells_y, cells_z = vel.shape
    lane = lax.broadcasted_iota(jnp.int32, (cells_y, cells_z), 1)

    def plane(x, acc):
        here = lane == x
        rolled = [
            pltpu.roll(vel[comp, x], lax.rem(x + last, cells_z), 1)
            for last in range(2)
            for comp in (0, 1)
        ]
        for i, comp in enumerate((0, 2)):
            y_faces[0, i, pl.ds(x, 1), :] = vel[comp, x, 0:1]
            y_faces[1, i, pl.ds(x, 1), :] = vel[comp, x, cells_y - 1 : cells_y]
        return tuple(jnp.where(here, new, old) for new, old in zip(rolled, acc))

    zero = jnp.zeros((cells_y, cells_z), jnp.float32)
    columns = lax.fori_loop(0, cells_x, plane, (zero,) * 4, unroll=4)
    for last in range(2):
        for i in range(2):
            z_faces[last, i] = columns[2 * last + i]

    t = targets[...]
    rows, lanes = t.shape
    shape = (lanes, lanes)
    upper = (
        lax.broadcasted_iota(jnp.int32, shape, 0) < lax.broadcasted_iota(jnp.int32, shape, 1)
    ).astype(jnp.float32).astype(jnp.bfloat16)
    square = (rows, rows)
    lower = (
        lax.broadcasted_iota(jnp.int32, square, 1) < lax.broadcasted_iota(jnp.int32, square, 0)
    ).astype(jnp.float32).astype(jnp.bfloat16)

    def body(w, acc):
        mine = t == w
        ones = mine.astype(jnp.float32).astype(jnp.bfloat16)
        inner = jnp.dot(ones, upper, preferred_element_type=jnp.float32)
        before = jnp.dot(lower, ones, preferred_element_type=jnp.float32)
        rank = inner + jnp.sum(before, axis=1, keepdims=True)
        return jnp.where(mine, w * capacity + rank.astype(jnp.int32), acc)

    slots[...] = lax.fori_loop(0, writers, body, jnp.zeros_like(t), unroll=8)


def halo_kernel(sizes, vel, y_faces, z_faces, halos, send_sem, recv_sem):
    place = [lax.axis_index(axis) for axis in ("gx", "gy", "wa")]
    cells_x = vel.shape[1]

    def beside(axis, step):
        size = sizes[axis]
        moved = lax.rem(place[axis] + step + size, size)
        return tuple(moved if i == axis else p for i, p in enumerate(place))

    across, along = pl.ds(0, vel.shape[2]), pl.ds(0, cells_x)
    moves = [
        (vel.at[pl.ds(1, 2), cells_x - 1], halos.at[0, :, across], beside(0, 1)),
        (vel.at[pl.ds(1, 2), 0], halos.at[1, :, across], beside(0, -1)),
        (y_faces.at[1], halos.at[2, :, along], beside(1, 1)),
        (y_faces.at[0], halos.at[3, :, along], beside(1, -1)),
        (z_faces.at[1], halos.at[4, :, across], beside(2, 1)),
        (z_faces.at[0], halos.at[5, :, across], beside(2, -1)),
    ]
    barrier = pltpu.get_barrier_semaphore()
    for _, _, device in moves:
        pl.semaphore_signal(barrier, inc=1, device_id=device, device_id_type=MESH)
    pl.semaphore_wait(barrier, len(moves))
    copies = []
    for k, (src, dst, device) in enumerate(moves):
        copy = pltpu.make_async_remote_copy(
            src_ref=src,
            dst_ref=dst,
            send_sem=send_sem.at[k],
            recv_sem=recv_sem.at[k],
            device_id=device,
            device_id_type=MESH,
        )
        copy.start()
        copies.append(copy)
    for copy in copies:
        copy.wait()


def block_rows(plane):
    cells_y, cells_z = plane.shape
    tiles = plane.reshape(cells_y // BY, BY, cells_z)
    sub = lax.broadcasted_iota(jnp.int32, tiles.shape, 1)
    group = lax.broadcasted_iota(jnp.int32, tiles.shape, 2) // BZ
    k = 1
    while k < BY:
        s_bit, g_bit = (sub & k) != 0, (group & k) != 0
        fwd = pltpu.roll(pltpu.roll(tiles, BY - k, 1), k * BZ, 2)
        back = pltpu.roll(pltpu.roll(tiles, k, 1), cells_z - k * BZ, 2)
        tiles = jnp.where(s_bit == g_bit, tiles, jnp.where(g_bit, fwd, back))
        k *= 2
    return tiles.reshape(cells_y, cells_z)


def blocks_kernel(slots, lens, vel, halos, table, out, squares, coeffs):
    comps, cells_x, cells_y, cells_z = vel.shape
    nblk = coeffs.shape[1]
    per_plane = nblk // cells_x
    rows = out.shape[0] // comps
    width = out.shape[1]
    row = lax.broadcasted_iota(jnp.int32, (cells_y, cells_z), 0)
    lane = lax.broadcasted_iota(jnp.int32, (cells_y, cells_z), 1)
    chunk = 128

    def clear(i, _):
        out[pl.ds(pl.multiple_of(i * chunk, chunk), chunk), :] = jnp.zeros(
            (chunk, width), jnp.float32
        )
        return 0

    lax.fori_loop(0, out.shape[0] // chunk, clear, 0)

    def plane(x, acc):
        u, v, w = vel[0, x], vel[1, x], vel[2, x]

        def along_x(comp):
            nxt = jnp.where(
                x == cells_x - 1, halos[1, comp - 1, :cells_y], vel[comp, jnp.minimum(x + 1, cells_x - 1)]
            )
            prv = jnp.where(x == 0, halos[0, comp - 1, :cells_y], vel[comp, jnp.maximum(x - 1, 0)])
            return (nxt - prv) * 0.5

        def along_y(f, face):
            nxt = jnp.where(
                row == cells_y - 1, halos[3, face, pl.ds(x, 1), :], pltpu.roll(f, cells_y - 1, 0)
            )
            prv = jnp.where(row == 0, halos[2, face, pl.ds(x, 1), :], pltpu.roll(f, 1, 0))
            return (nxt - prv) * 0.5

        def along_z(f, face):
            after = pltpu.roll(halos[5, face, :cells_y], cells_z - 1 - x, 1)
            before = pltpu.roll(halos[4, face, :cells_y], lax.rem(cells_z - x, cells_z), 1)
            nxt = jnp.where(lane == cells_z - 1, after, pltpu.roll(f, cells_z - 1, 1))
            prv = jnp.where(lane == 0, before, pltpu.roll(f, 1, 1))
            return (nxt - prv) * 0.5

        curl = (
            along_y(w, 1) - along_z(v, 1),
            along_z(u, 0) - along_x(2),
            along_x(1) - along_y(u, 0),
        )
        for c in curl:
            acc = acc + jnp.sum((c * c).reshape(cells_y // 8, 8, cells_z), axis=0)
        flat = jnp.concatenate([block_rows(c) for c in curl], axis=0)
        high = flat.astype(jnp.bfloat16)
        low = (flat - high.astype(jnp.float32)).astype(jnp.bfloat16)
        both = jnp.dot(
            jnp.concatenate([high, low], axis=1), table[...], preferred_element_type=jnp.float32
        )
        result = both[:, :width] + both[:, width:]
        start = pl.multiple_of(x * per_plane, 8)
        for c in range(comps):
            coeffs[c, pl.ds(start, per_plane), :] = result[c * per_plane : (c + 1) * per_plane]
        return acc

    freqs = lax.broadcasted_iota(jnp.int32, (1, width), 1)
    group = 8

    def place(x):
        for start in range(0, per_plane, group):
            found = []
            for k in range(start, min(start + group, per_plane)):
                i = x * per_plane + k
                keep = freqs < lens[i]
                for c in range(comps):
                    cut = jnp.where(keep, coeffs[c, pl.ds(i, 1), :], 0.0)
                    found.append((c * rows + slots[i], cut))
            for spot, cut in found:
                out[pl.ds(spot, 1), :] = cut

    together = next(n for n in (UNROLL, 2, 1) if cells_x % n == 0)

    def step(t, acc):
        for k in range(together):
            place((t - 1) * together + k)
        return planes(t, acc)

    def planes(t, acc):
        for k in range(together):
            acc = plane(t * together + k, acc)
        return acc

    first = planes(0, jnp.zeros((8, cells_z), jnp.float32))
    squares[...] = lax.fori_loop(1, cells_x // together, step, first)
    for k in range(together):
        place(cells_x - together + k)


def exchange_kernel(
    n_x, n_y, n_z, send, squares, recv, total, near, far, send_sem, recv_sem, part_send, part_recv,
    own_sem,
):
    a, b = lax.axis_index("gx"), lax.axis_index("gy")
    c = lax.axis_index("wa")
    me = a * n_y + b
    offsets = [(i, j) for i in range(n_x) for j in range(n_y) if i or j]
    offsets.sort(key=lambda o: (bool(o[0]) and bool(o[1]), min(o[1], n_y - o[1])))
    peers = [(lax.rem(a + i, n_x), lax.rem(b + j, n_y), c) for i, j in offsets]
    mates = [(a, b, lax.rem(c + k, n_z)) for k in range(1, n_z)]
    barrier = pltpu.get_barrier_semaphore()
    for device in mates + peers:
        pl.semaphore_signal(barrier, inc=1, device_id=device, device_id_type=MESH)
    pl.semaphore_wait(barrier, len(peers) + len(mates))

    def start(src, dst, sems, device):
        copy = pltpu.make_async_remote_copy(
            src_ref=src,
            dst_ref=dst,
            send_sem=sems[0],
            recv_sem=sems[1],
            device_id=device,
            device_id_type=MESH,
        )
        copy.start()
        return copy

    own = pltpu.make_async_copy(squares, near.at[c], own_sem)
    own.start()
    first = [
        start(squares, near.at[c], (part_send.at[k], part_recv.at[k]), device)
        for k, device in enumerate(mates)
    ]
    def blocks_to(k):
        device = peers[k]
        return start(
            send.at[:, device[0] * n_y + device[1]],
            recv.at[:, me],
            (send_sem.at[k], recv_sem.at[k]),
            device,
        )

    ahead = min(3, len(peers))
    copies = [blocks_to(k) for k in range(ahead)]
    own.wait()
    for copy in first:
        copy.wait()
    for k, device in enumerate(peers):
        sem = n_z - 1 + k
        copies.append(start(near, far.at[k], (part_send.at[sem], part_recv.at[sem]), device))
    copies += [blocks_to(k) for k in range(ahead, len(peers))]
    for copy in copies:
        copy.wait()
    total[...] = jnp.sum(near[...], axis=0) + jnp.sum(far[...], axis=(0, 1))


def scale_kernel(every, me, squares, recv, send, out):
    total = jnp.sum(squares[...], keepdims=True)
    scale = 1.0 / jnp.sqrt(total / every + 1e-06)
    own = pl.program_id(0) == me[0]

    @pl.when(own)
    def _():
        out[...] = send[...] * scale[None, None]

    @pl.when(jnp.logical_not(own))
    def _():
        out[...] = recv[...] * scale[None, None]


def local(velocity, lengths, destinations):
    n_x, n_y, n_z = lax.axis_size("gx"), lax.axis_size("gy"), lax.axis_size("wa")
    comps, cells_x, cells_y, cells_z = velocity.shape
    width = BY * BZ
    nblk = cells_x * cells_y * cells_z // width
    writers = n_x * n_y
    capacity = max(2, 2 * nblk // writers)
    f32 = jnp.float32

    smem = pl.BlockSpec(memory_space=pltpu.SMEM)
    vmem = pl.BlockSpec(memory_space=pltpu.VMEM)
    anywhere = pl.BlockSpec(memory_space=pl.ANY)
    slots, y_faces, z_faces = pl.pallas_call(
        functools.partial(faces_kernel, writers, capacity),
        out_shape=(
            jax.ShapeDtypeStruct((nblk // 128, 128), jnp.int32),
            jax.ShapeDtypeStruct((2, 2, cells_x, cells_z), f32),
            jax.ShapeDtypeStruct((2, 2, cells_y, cells_z), f32),
        ),
        name="faces",
    )(destinations.reshape(nblk // 128, 128), velocity)
    halos = pl.pallas_call(
        functools.partial(halo_kernel, (n_x, n_y, n_z)),
        out_shape=jax.ShapeDtypeStruct((6, 2, max(cells_x, cells_y), cells_z), f32),
        in_specs=[anywhere] * 3,
        out_specs=anywhere,
        scratch_shapes=[pltpu.SemaphoreType.DMA((6,)), pltpu.SemaphoreType.DMA((6,))],
        compiler_params=pltpu.CompilerParams(collective_id=1, has_side_effects=True),
        name="halo",
    )(velocity, y_faces, z_faces)

    table = jnp.asarray(split_table())
    outgoing, squares = pl.pallas_call(
        blocks_kernel,
        out_shape=(
            jax.ShapeDtypeStruct((comps * writers * capacity, width), f32),
            jax.ShapeDtypeStruct((8, cells_z), f32),
        ),
        in_specs=[smem, smem] + [vmem] * 3,
        out_specs=(vmem, vmem),
        scratch_shapes=[pltpu.VMEM((comps, nblk, width), f32)],
        compiler_params=pltpu.CompilerParams(vmem_limit_bytes=48 * 2**20),
        name="blocks",
    )(slots.reshape(nblk), lengths.reshape(nblk), velocity, halos, table)
    outgoing = outgoing.reshape(comps, writers, capacity, width)

    arrived, squares = pl.pallas_call(
        functools.partial(exchange_kernel, n_x, n_y, n_z),
        out_shape=(
            jax.ShapeDtypeStruct(outgoing.shape, f32),
            jax.ShapeDtypeStruct(squares.shape, f32),
        ),
        in_specs=[anywhere, vmem],
        out_specs=(anywhere, vmem),
        scratch_shapes=[
            pltpu.VMEM((n_z,) + squares.shape, f32),
            pltpu.VMEM((writers - 1, n_z) + squares.shape, f32),
            pltpu.SemaphoreType.DMA((writers - 1,)),
            pltpu.SemaphoreType.DMA((writers - 1,)),
            pltpu.SemaphoreType.DMA((writers + n_z - 2,)),
            pltpu.SemaphoreType.DMA((writers + n_z - 2,)),
            pltpu.SemaphoreType.DMA,
        ],
        compiler_params=pltpu.CompilerParams(collective_id=0, has_side_effects=True),
        name="exchange",
    )(outgoing, squares)

    every = velocity.size * n_x * n_y * n_z
    me = (lax.axis_index("gx") * n_y + lax.axis_index("gy")).astype(jnp.int32).reshape(1)
    block = (comps, 1, capacity, width)
    received = pl.pallas_call(
        functools.partial(scale_kernel, float(every)),
        grid_spec=pltpu.PrefetchScalarGridSpec(
            num_scalar_prefetch=1,
            grid=(writers,),
            in_specs=[
                pl.BlockSpec((8, cells_z), lambda s, me: (0, 0)),
                pl.BlockSpec(block, lambda s, me: (0, s, 0, 0)),
                pl.BlockSpec(block, lambda s, me: (0, me[0], 0, 0)),
            ],
            out_specs=pl.BlockSpec(block, lambda s, me: (0, s, 0, 0)),
        ),
        out_shape=jax.ShapeDtypeStruct(outgoing.shape, f32),
        name="scale",
    )(me, squares, arrived, outgoing)
    return received.reshape(1, 1, comps, writers, capacity, width)


def solution(mesh):
    return jax.shard_map(
        local,
        mesh=mesh,
        in_specs=(
            P(None, "gx", "gy", "wa"),
            P("gx", "gy", "wa", None),
            P("gx", "gy", "wa", None, None),
        ),
        out_specs=P(("gx", "gy"), "wa", None, None, None, None),
        check_vma=False,
    )
```

profile of v0, /device:TPU:0, one launch (start us, length us, event | category | flops | bytes accessed | tf_op | source)
XLA Modules:
  0.0 187.3 jit_solution(17109411906843809271)
XLA Ops:
  0.0 0.0 copy-start.2
  0.0 0.0 copy-start
  0.0 0.0 copy-start.3
  0.0 4.6 %faces.1 = (s32[16,128]{1,0:T(8,128)}, f32[2,2,32,128]{3,2,1,0:T(8,128)}, f32[2,2,64,128]{3,2,1,0:T(8,128)}) custom-call(s32[16,128]{1,0:T(8,128)} %bitcast.10, f32[3,32,64,128]{3,2,1,0:T(8,128)} %vel.5), custom_call_target="tpu_custom_call" | custom-call | tf_op jit(solution)/shard_map/faces/pallas_call | solution.py:304
  4.6 10.2 %halo.1.halos = f32[6,2,64,128]{3,2,1,0:T(8,128)} custom-call(f32[3,32,64,128]{3,2,1,0:T(8,128)} %vel.5, f32[2,2,32,128]{3,2,1,0:T(8,128)} %get-tuple-element.13.y_faces, f32[2,2,64,128]{3,2,1,0:T(8,128)} %get-tuple-element.14.z_faces), custom_call_target="tpu_custom_call" | custom-call | tf_op jit(solution)/shard_map/halo/pallas_call | solution.py:313
  14.8 0.0 copy-done.2
  14.8 0.0 copy-done
  14.8 0.0 copy-done.3
  14.8 0.0 copy-start.1
  14.9 1.0 copy-done.1
  15.8 0.0 copy-start.4
  15.8 0.7 copy-done.4
  16.5 17.8 %blocks.1 = (f32[12288,128]{1,0:T(8,128)}, f32[8,128]{1,0:T(8,128)S(1)}) custom-call(s32[2048]{0:T(1024)S(1)} %bitcast.7, s32[2048]{0:T(1024)S(1)} %bitcast.6, f32[3,32,64,128]{3,2,1,0:T(8,128)S(1)} %copy-done, f32[6,2,64,128]{3,2,1,0:T(8,128)S(1)} %copy-done.1, bf16[256,256]{1,0:T(8,128)(2,1)S(1)} %copy-done.2), custom_call_target="tpu_custom_call" | custom-call | tf_op jit(solution)/shard_map/blocks/pallas_call | solution.py:324
  34.3 0.0 copy-start.5
  34.3 0.6 copy-done.5
  34.9 143.8 %exchange.1 = (f32[3,8,512,128]{3,2,1,0:T(8,128)}, f32[8,128]{1,0:T(8,128)}) custom-call(f32[3,8,512,128]{3,2,1,0:T(8,128)} %bitcast.8, f32[8,128]{1,0:T(8,128)} %copy-done.5), custom_call_target="tpu_custom_call" | custom-call | tf_op jit(solution)/shard_map/exchange/pallas_call | solution.py:338
  178.7 8.6 %scale.1 = f32[3,8,512,128]{3,2,1,0:T(8,128)} custom-call(s32[1]{0:T(128)} %bitcast.me, f32[8,128]{1,0:T(8,128)} %get-tuple-element.17.squares, f32[3,8,512,128]{3,2,1,0:T(8,128)} %get-tuple-element.18.recv, f32[3,8,512,128]{3,2,1,0:T(8,128)} %bitcast.9), custom_call_target="tpu_custom_call" | custom-call | tf_op jit(solution)/shard_map/scale/pallas_call | solution.py:362
Async XLA Ops:
  0.0 14.8 %copy-start.2 = (bf16[256,256]{1,0:T(8,128)(2,1)S(1)}, bf16[256,256]{1,0:T(8,128)(2,1)}, u32[]{:S(2)}) copy-start(bf16[256,256]{1,0:T(8,128)(2,1)} %constant.15.clone.table) | copy-start | bytes 393220
  0.0 14.8 %copy-start = (f32[3,32,64,128]{3,2,1,0:T(8,128)S(1)}, f32[3,32,64,128]{3,2,1,0:T(8,128)}, u32[]{:S(2)}) copy-start(f32[3,32,64,128]{3,2,1,0:T(8,128)} %vel.5) | copy-start | bytes 9437188
  0.0 14.8 %copy-start.3 = (s32[1,1,1,2048]{3,2,1,0:T(1,128)S(1)}, s32[1,1,1,2048]{3,2,1,0:T(1,128)}, u32[]{:S(2)}) copy-start(s32[1,1,1,2048]{3,2,1,0:T(1,128)} %param.5) | copy-start | bytes 24580
  14.8 1.0 copy-start.1
  15.8 0.7 copy-start.4
  34.3 0.6 copy-start.5
where the time goes:
time: 188 us; the launch traced here: 187 us
  Pallas kernels  185 us (98%)
  local copies, waits for them, and re-layouts  2.29 us (1%)
    pallas_call x1, Pallas kernels, local(): pl.pallas_call(functools.partial(exchange_kernel, n_x, n_y, n_z), out_sha...  144 us
    pallas_call x1, Pallas kernels, local(): pl.pallas_call(blocks_kernel, out_shape=(jax.ShapeDtypeStruct((comps * wr...  17.8 us
    pallas_call x1, Pallas kernels, local(): pl.pallas_call(functools.partial(halo_kernel, (n_x, n_y, n_z)), out_shape...  10.2 us
    pallas_call x1, Pallas kernels, local(): pl.pallas_call(functools.partial(scale_kernel, float(every)), grid_spec=p...  8.57 us
    pallas_call x1, Pallas kernels, local(): pl.pallas_call(functools.partial(faces_kernel, writers, capacity), out_sh...  4.58 us

commit v1 on v0

v1 whole, which is shorter than its diff:
```python
import functools

import jax
import jax.numpy as jnp
import numpy as np
from jax import lax
from jax.experimental import pallas as pl
from jax.experimental.pallas import tpu as pltpu
from jax.sharding import PartitionSpec as P

BY = 8
BZ = 16
UNROLL = 2
MESH = pl.DeviceIdType.MESH


def dct_table(count):
    freqs, points = np.arange(count)[:, None], np.arange(count)[None, :]
    table = np.cos(np.pi * (points + 0.5) * freqs / count) * np.sqrt(2.0 / count)
    return np.where(freqs == 0, table * np.sqrt(0.5), table)


def split_table():
    kron = np.kron(dct_table(BY), dct_table(BZ)).T.astype(np.float32)
    high = kron.astype(jnp.bfloat16)
    low = (kron - high.astype(np.float32)).astype(jnp.bfloat16)
    return np.block([[high, low], [high, np.zeros_like(low)]]).astype(jnp.bfloat16)


def faces_kernel(
    writers, capacity, pitch, targets, lens, vel, words, spots, blank, y_faces, z_faces, need
):
    comps, cells_x, cells_y, cells_z = vel.shape
    lane = lax.broadcasted_iota(jnp.int32, (cells_y, cells_z), 1)

    def plane(x, acc):
        here = lane == x
        rolled = [
            pltpu.roll(vel[comp, x], lax.rem(x + last, cells_z), 1)
            for last in range(2)
            for comp in (0, 1)
        ]
        for i, comp in enumerate((0, 2)):
            y_faces[0, i, pl.ds(x, 1), :] = vel[comp, x, 0:1]
            y_faces[1, i, pl.ds(x, 1), :] = vel[comp, x, cells_y - 1 : cells_y]
        return tuple(jnp.where(here, new, old) for new, old in zip(rolled, acc))

    zero = jnp.zeros((cells_y, cells_z), jnp.float32)
    columns = lax.fori_loop(0, cells_x, plane, (zero,) * 4, unroll=4)
    for last in range(2):
        for i in range(2):
            z_faces[last, i] = columns[2 * last + i]

    t, kept = targets[...], lens[...]
    rows, lanes = t.shape
    shape = (lanes, lanes)
    upper = (
        lax.broadcasted_iota(jnp.int32, shape, 0) < lax.broadcasted_iota(jnp.int32, shape, 1)
    ).astype(jnp.float32).astype(jnp.bfloat16)
    square = (rows, rows)
    lower = (
        lax.broadcasted_iota(jnp.int32, square, 1) < lax.broadcasted_iota(jnp.int32, square, 0)
    ).astype(jnp.float32).astype(jnp.bfloat16)
    weight = kept.astype(jnp.float32)

    def body(w, acc):
        spot, start, most = acc
        mine = t == w
        ones = mine.astype(jnp.float32)
        sizes = jnp.where(mine, weight, 0.0)
        both = jnp.concatenate([ones, sizes], axis=0).astype(jnp.bfloat16)
        inner = jnp.dot(both, upper, preferred_element_type=jnp.float32)
        side = jnp.concatenate([ones, sizes], axis=1).astype(jnp.bfloat16)
        before = jnp.dot(lower, side, preferred_element_type=jnp.float32)
        rank = inner[:rows] + jnp.sum(before[:, :lanes], axis=1, keepdims=True)
        offset = inner[rows:] + jnp.sum(before[:, lanes:], axis=1, keepdims=True)
        spot = jnp.where(mine, w * capacity + rank.astype(jnp.int32), spot)
        start = jnp.where(mine, w * pitch + offset.astype(jnp.int32), start)
        most = jnp.where(mine, offset + weight, most)
        return spot, start, most

    none = jnp.zeros_like(t)
    spot, start, most = lax.fori_loop(
        0, writers, body, (none, none, jnp.zeros(t.shape, jnp.float32)), unroll=8
    )
    spots[...] = spot
    words[...] = start * 256 + kept
    need[...] = jnp.max(most.reshape(rows // 8, 8, lanes), axis=0)
    place = lax.broadcasted_iota(jnp.int32, blank.shape, 0) * lanes + lax.broadcasted_iota(
        jnp.int32, blank.shape, 1
    )
    blank[...] = lax.div(place, capacity) * (pitch * 256)


def plane_peers(n_x, n_y):
    a, b, c = (lax.axis_index(axis) for axis in ("gx", "gy", "wa"))
    offsets = [(i, j) for i in range(n_x) for j in range(n_y) if i or j]
    offsets.sort(key=lambda o: (bool(o[0]) and bool(o[1]), min(o[1], n_y - o[1])))
    return [(lax.rem(a + i, n_x), lax.rem(b + j, n_y), c) for i, j in offsets]


def line_mates(n_z):
    a, b, c = (lax.axis_index(axis) for axis in ("gx", "gy", "wa"))
    return [(a, b, lax.rem(c + k, n_z)) for k in range(1, n_z)]


def send_to(src, dst, send_sem, recv_sem, device):
    copy = pltpu.make_async_remote_copy(
        src_ref=src,
        dst_ref=dst,
        send_sem=send_sem,
        recv_sem=recv_sem,
        device_id=device,
        device_id_type=MESH,
    )
    copy.start()
    return copy


def halo_kernel(
    sizes, tiers, vel, y_faces, z_faces, need, halos, tier, near, far, send_sem, recv_sem, part_send,
    part_recv, own_sem,
):
    place = [lax.axis_index(axis) for axis in ("gx", "gy", "wa")]
    n_x, n_y, n_z = sizes
    cells_x = vel.shape[1]

    def beside(axis, step):
        size = sizes[axis]
        moved = lax.rem(place[axis] + step + size, size)
        return tuple(moved if i == axis else p for i, p in enumerate(place))

    across, along = pl.ds(0, vel.shape[2]), pl.ds(0, cells_x)
    moves = [
        (vel.at[pl.ds(1, 2), cells_x - 1], halos.at[0, :, across], beside(0, 1)),
        (vel.at[pl.ds(1, 2), 0], halos.at[1, :, across], beside(0, -1)),
        (y_faces.at[1], halos.at[2, :, along], beside(1, 1)),
        (y_faces.at[0], halos.at[3, :, along], beside(1, -1)),
        (z_faces.at[1], halos.at[4, :, across], beside(2, 1)),
        (z_faces.at[0], halos.at[5, :, across], beside(2, -1)),
    ]
    peers, mates = plane_peers(n_x, n_y), line_mates(n_z)
    others = [device for _, _, device in moves] + peers + mates
    barrier = pltpu.get_barrier_semaphore()
    for device in others:
        pl.semaphore_signal(barrier, inc=1, device_id=device, device_id_type=MESH)
    pl.semaphore_wait(barrier, len(others))
    c = place[2]
    own = pltpu.make_async_copy(need, near.at[c], own_sem)
    own.start()
    first = [
        send_to(need, near.at[c], part_send.at[k], part_recv.at[k], device)
        for k, device in enumerate(mates)
    ]
    copies = [
        send_to(src, dst, send_sem.at[k], recv_sem.at[k], device)
        for k, (src, dst, device) in enumerate(moves)
    ]
    own.wait()
    for copy in first:
        copy.wait()
    for k, device in enumerate(peers):
        sem = n_z - 1 + k
        copies.append(send_to(near, far.at[k], part_send.at[sem], part_recv.at[sem], device))
    for copy in copies:
        copy.wait()
    most = jnp.maximum(jnp.max(near[...], axis=0), jnp.max(far[...], axis=(0, 1)))
    above = jnp.max(most)
    tier[0] = sum((above > 128.0 * rows).astype(jnp.int32) for rows in tiers[:-1])


def block_rows(plane):
    cells_y, cells_z = plane.shape
    tiles = plane.reshape(cells_y // BY, BY, cells_z)
    sub = lax.broadcasted_iota(jnp.int32, tiles.shape, 1)
    group = lax.broadcasted_iota(jnp.int32, tiles.shape, 2) // BZ
    k = 1
    while k < BY:
        s_bit, g_bit = (sub & k) != 0, (group & k) != 0
        fwd = pltpu.roll(pltpu.roll(tiles, BY - k, 1), k * BZ, 2)
        back = pltpu.roll(pltpu.roll(tiles, k, 1), cells_z - k * BZ, 2)
        tiles = jnp.where(s_bit == g_bit, tiles, jnp.where(g_bit, fwd, back))
        k *= 2
    return tiles.reshape(cells_y, cells_z)


def blocks_kernel(words, spots, blank, vel, halos, table, out, squares, meta, coeffs, meta_sem):
    comps, cells_x, cells_y, cells_z = vel.shape
    nblk = coeffs.shape[0] // comps
    per_plane = nblk // cells_x
    width = out.shape[1]
    row = lax.broadcasted_iota(jnp.int32, (cells_y, cells_z), 0)
    lane = lax.broadcasted_iota(jnp.int32, (cells_y, cells_z), 1)
    clear = pltpu.make_async_copy(blank, meta, meta_sem)
    clear.start()

    def plane(x, acc):
        u, v, w = vel[0, x], vel[1, x], vel[2, x]

        def along_x(comp):
            nxt = jnp.where(
                x == cells_x - 1, halos[1, comp - 1, :cells_y], vel[comp, jnp.minimum(x + 1, cells_x - 1)]
            )
            prv = jnp.where(x == 0, halos[0, comp - 1, :cells_y], vel[comp, jnp.maximum(x - 1, 0)])
            return (nxt - prv) * 0.5

        def along_y(f, face):
            nxt = jnp.where(
                row == cells_y - 1, halos[3, face, pl.ds(x, 1), :], pltpu.roll(f, cells_y - 1, 0)
            )
            prv = jnp.where(row == 0, halos[2, face, pl.ds(x, 1), :], pltpu.roll(f, 1, 0))
            return (nxt - prv) * 0.5

        def along_z(f, face):
            after = pltpu.roll(halos[5, face, :cells_y], cells_z - 1 - x, 1)
            before = pltpu.roll(halos[4, face, :cells_y], lax.rem(cells_z - x, cells_z), 1)
            nxt = jnp.where(lane == cells_z - 1, after, pltpu.roll(f, cells_z - 1, 1))
            prv = jnp.where(lane == 0, before, pltpu.roll(f, 1, 1))
            return (nxt - prv) * 0.5

        curl = (
            along_y(w, 1) - along_z(v, 1),
            along_z(u, 0) - along_x(2),
            along_x(1) - along_y(u, 0),
        )
        for c in curl:
            acc = acc + jnp.sum((c * c).reshape(cells_y // 8, 8, cells_z), axis=0)
        flat = jnp.concatenate([block_rows(c) for c in curl], axis=0)
        high = flat.astype(jnp.bfloat16)
        low = (flat - high.astype(jnp.float32)).astype(jnp.bfloat16)
        both = jnp.dot(
            jnp.concatenate([high, low], axis=1), table[...], preferred_element_type=jnp.float32
        )
        result = both[:, :width] + both[:, width:]
        start = x * (comps * per_plane)
        for c in range(comps):
            coeffs[pl.ds(start + c, per_plane, stride=comps), :] = result[
                c * per_plane : (c + 1) * per_plane
            ]
        return acc

    spread = lax.broadcasted_iota(jnp.int32, (comps, width), 1)
    group = 8

    def place(x):
        for start in range(0, per_plane, group):
            found = []
            for k in range(start, min(start + group, per_plane)):
                i = x * per_plane + k
                word = words[i]
                meta[spots[i]] = word
                shift = lax.shift_right_logical(word, 8) & (width - 1)
                row = lax.shift_right_logical(word, 15) * comps
                moved = pltpu.roll(coeffs[pl.ds(i * comps, comps), :], shift, 1)
                found.append((row, moved, spread >= shift))
            for row, moved, mask in found:
                pltpu.store(out.at[pl.ds(row, comps), :], moved, mask=mask)
                out[pl.ds(row + comps, comps), :] = moved

    together = next(n for n in (UNROLL, 2, 1) if cells_x % n == 0)

    def step(t, acc):
        for k in range(together):
            place((t - 1) * together + k)
        return planes(t, acc)

    def planes(t, acc):
        for k in range(together):
            acc = plane(t * together + k, acc)
        return acc

    clear.wait()
    first = planes(0, jnp.zeros((8, cells_z), jnp.float32))
    squares[...] = lax.fori_loop(1, cells_x // together, step, first)
    for k in range(together):
        place(cells_x - together + k)


def exchange_kernel(
    n_x, n_y, n_z, rows, send, squares, meta, recv, total, heard, near, far, send_sem, recv_sem,
    part_send, part_recv, word_send, word_recv, own_sem,
):
    a, b = lax.axis_index("gx"), lax.axis_index("gy")
    c = lax.axis_index("wa")
    me = a * n_y + b
    peers, mates = plane_peers(n_x, n_y), line_mates(n_z)
    barrier = pltpu.get_barrier_semaphore()
    for device in mates + peers:
        pl.semaphore_signal(barrier, inc=1, device_id=device, device_id_type=MESH)
    pl.semaphore_wait(barrier, len(peers) + len(mates))
    used = pl.ds(0, rows)

    own = [
        pltpu.make_async_copy(squares, near.at[c], own_sem.at[0]),
        pltpu.make_async_copy(meta.at[me], heard.at[me], own_sem.at[1]),
        pltpu.make_async_copy(send.at[me, used], recv.at[me, used], own_sem.at[2]),
    ]
    for copy in own:
        copy.start()
    first = [
        send_to(squares, near.at[c], part_send.at[k], part_recv.at[k], device)
        for k, device in enumerate(mates)
    ]

    def number(device):
        return device[0] * n_y + device[1]

    def blocks_to(k):
        device = peers[k]
        return send_to(
            send.at[number(device), used], recv.at[me, used], send_sem.at[k], recv_sem.at[k], device
        )

    copies = [
        send_to(meta.at[number(device)], heard.at[me], word_send.at[k], word_recv.at[k], device)
        for k, device in enumerate(peers)
    ]
    ahead = min(3, len(peers))
    copies += [blocks_to(k) for k in range(ahead)]
    own[0].wait()
    for copy in first:
        copy.wait()
    for k, device in enumerate(peers):
        sem = n_z - 1 + k
        copies.append(send_to(near, far.at[k], part_send.at[sem], part_recv.at[sem], device))
    copies += [blocks_to(k) for k in range(ahead, len(peers))]
    for copy in own[1:]:
        copy.wait()
    for copy in copies:
        copy.wait()
    total[...] = jnp.sum(near[...], axis=0) + jnp.sum(far[...], axis=(0, 1))


def unpack_kernel(every, n_y, pitch, meta, squares, recv, out, scale):
    comps, _, capacity, width = out.shape
    source = pl.program_id(0)
    base = (lax.axis_index("gx") * n_y + lax.axis_index("gy")) * pitch

    @pl.when(source == 0)
    def _():
        total = jnp.sum(squares[...], keepdims=True)
        scale[...] = jnp.broadcast_to(1.0 / jnp.sqrt(total / every + 1e-06), scale.shape)

    lane = lax.broadcasted_iota(jnp.int32, (comps, width), 1)
    factor = scale[:comps]
    group = 16 if capacity % 16 == 0 else 8

    def some(t, _):
        found = []
        for k in range(group):
            slot = t * group + k
            word = meta[source * capacity + slot]
            length = word & 255
            shift = lax.shift_right_logical(word, 8) & (width - 1)
            row = (lax.shift_right_logical(word, 15) - base) * comps
            head = recv[0, pl.ds(row, comps), :]
            tail = recv[0, pl.ds(row + comps, comps), :]
            joined = jnp.where(lane >= shift, head, tail)
            moved = pltpu.roll(joined, (width - shift) & (width - 1), 1)
            found.append((slot, jnp.where(lane < length, moved * factor, 0.0)))
        for slot, value in found:
            for c in range(comps):
                out[c, 0, pl.ds(slot, 1), :] = value[c : c + 1]
        return 0

    lax.fori_loop(0, capacity // group, some, 0)


def tier_rows(capacity):
    steps = (16, 18, 19, 20, 22, 24, 28, 32)
    return sorted({-(-capacity * step // (32 * 8)) * 8 for step in steps})


def local(velocity, lengths, destinations):
    n_x, n_y, n_z = lax.axis_size("gx"), lax.axis_size("gy"), lax.axis_size("wa")
    comps, cells_x, cells_y, cells_z = velocity.shape
    width = BY * BZ
    nblk = cells_x * cells_y * cells_z // width
    writers = n_x * n_y
    capacity = max(2, 2 * nblk // writers)
    region = capacity + 8
    f32 = jnp.float32
    tiers = tier_rows(capacity)

    smem = pl.BlockSpec(memory_space=pltpu.SMEM)
    vmem = pl.BlockSpec(memory_space=pltpu.VMEM)
    anywhere = pl.BlockSpec(memory_space=pl.ANY)
    dma = pltpu.SemaphoreType.DMA
    flat = jax.ShapeDtypeStruct((nblk // 128, 128), jnp.int32)
    words, spots, blank, y_faces, z_faces, need = pl.pallas_call(
        functools.partial(faces_kernel, writers, capacity, region * width),
        out_shape=(
            flat,
            flat,
            jax.ShapeDtypeStruct((writers * capacity // 128, 128), jnp.int32),
            jax.ShapeDtypeStruct((2, 2, cells_x, cells_z), f32),
            jax.ShapeDtypeStruct((2, 2, cells_y, cells_z), f32),
            jax.ShapeDtypeStruct((8, 128), f32),
        ),
        name="faces",
    )(destinations.reshape(nblk // 128, 128), lengths.reshape(nblk // 128, 128), velocity)
    halos, tier = pl.pallas_call(
        functools.partial(halo_kernel, (n_x, n_y, n_z), tiers),
        out_shape=(
            jax.ShapeDtypeStruct((6, 2, max(cells_x, cells_y), cells_z), f32),
            jax.ShapeDtypeStruct((1,), jnp.int32),
        ),
        in_specs=[anywhere] * 3 + [vmem],
        out_specs=(anywhere, smem),
        scratch_shapes=[
            pltpu.VMEM((n_z,) + need.shape, f32),
            pltpu.VMEM((writers - 1, n_z) + need.shape, f32),
            dma((6,)),
            dma((6,)),
            dma((writers + n_z - 2,)),
            dma((writers + n_z - 2,)),
            dma,
        ],
        compiler_params=pltpu.CompilerParams(collective_id=1, has_side_effects=True),
        name="halo",
    )(velocity, y_faces, z_faces, need)

    table = jnp.asarray(split_table())
    outgoing, squares, meta = pl.pallas_call(
        blocks_kernel,
        out_shape=(
            jax.ShapeDtypeStruct((writers * region * comps, width), f32),
            jax.ShapeDtypeStruct((8, cells_z), f32),
            jax.ShapeDtypeStruct((writers * capacity,), jnp.int32),
        ),
        in_specs=[smem, smem] + [anywhere] + [vmem] * 3,
        out_specs=(vmem, vmem, smem),
        scratch_shapes=[pltpu.VMEM((nblk * comps, width), f32), dma],
        compiler_params=pltpu.CompilerParams(vmem_limit_bytes=48 * 2**20),
        name="blocks",
    )(
        words.reshape(nblk),
        spots.reshape(nblk),
        blank.reshape(writers * capacity),
        velocity,
        halos,
        table,
    )
    outgoing = outgoing.reshape(writers, region * comps, width)
    part = min(capacity, 128)
    meta = meta.reshape(writers, capacity // part, part)

    def exchange(index, outgoing, squares, meta):
        rows = tiers[index] * comps
        return pl.pallas_call(
            functools.partial(exchange_kernel, n_x, n_y, n_z, rows),
            out_shape=(
                jax.ShapeDtypeStruct(outgoing.shape, f32),
                jax.ShapeDtypeStruct(squares.shape, f32),
                jax.ShapeDtypeStruct(meta.shape, jnp.int32),
            ),
            in_specs=[anywhere, vmem, anywhere],
            out_specs=(anywhere, vmem, anywhere),
            scratch_shapes=[
                pltpu.VMEM((n_z,) + squares.shape, f32),
                pltpu.VMEM((writers - 1, n_z) + squares.shape, f32),
                dma((writers - 1,)),
                dma((writers - 1,)),
                dma((writers + n_z - 2,)),
                dma((writers + n_z - 2,)),
                dma((writers - 1,)),
                dma((writers - 1,)),
                dma((3,)),
            ],
            compiler_params=pltpu.CompilerParams(collective_id=2 + index, has_side_effects=True),
            name=f"exchange{tiers[index]}",
        )(outgoing, squares, meta)

    branches = [functools.partial(exchange, index) for index in range(len(tiers))]
    arrived, squares, heard = lax.switch(tier[0], branches, outgoing, squares, meta)

    every = velocity.size * n_x * n_y * n_z
    received = pl.pallas_call(
        functools.partial(unpack_kernel, float(every), n_y, region),
        grid=(writers,),
        in_specs=[
            smem,
            pl.BlockSpec((8, cells_z), lambda s: (0, 0)),
            pl.BlockSpec((1, region * comps, width), lambda s: (s, 0, 0)),
        ],
        out_specs=pl.BlockSpec((comps, 1, capacity, width), lambda s: (0, s, 0, 0)),
        out_shape=jax.ShapeDtypeStruct((comps, writers, capacity, width), f32),
        scratch_shapes=[pltpu.VMEM((8, width), f32)],
        name="unpack",
    )(heard.reshape(writers * capacity), squares, arrived)
    return received.reshape(1, 1, comps, writers, capacity, width)


def solution(mesh):
    return jax.shard_map(
        local,
        mesh=mesh,
        in_specs=(
            P(None, "gx", "gy", "wa"),
            P("gx", "gy", "wa", None),
            P("gx", "gy", "wa", None, None),
        ),
        out_specs=P(("gx", "gy"), "wa", None, None, None, None),
        check_vma=False,
    )
```

time: 188 us -> 166 us (0.88)
  Pallas kernels: 185 us -> 162 us
    pallas_call x5, Pallas kernels: 185 us -> 162 us  [the longest x1 88.2 us: exchange(): pl.pallas_call(functools.partial(exchange_kernel, n_x, n_y, n_z, rows), o...]
where the time goes in v1:
time: 166 us
  Pallas kernels  162 us (98%)
  local copies, waits for them, and re-layouts  3.11 us (2%)
    pallas_call x1, Pallas kernels, exchange(): pl.pallas_call(functools.partial(exchange_kernel, n_x, n_y, n_z, rows), o...  88.2 us
    pallas_call x1, Pallas kernels, local(): pl.pallas_call(functools.partial(unpack_kernel, float(every), n_y, region...  32 us
    pallas_call x1, Pallas kernels, local(): pl.pallas_call(blocks_kernel, out_shape=(jax.ShapeDtypeStruct((writers *...  22 us
    pallas_call x1, Pallas kernels, local(): pl.pallas_call(functools.partial(halo_kernel, (n_x, n_y, n_z), tiers), ou...  15.1 us
    pallas_call x1, Pallas kernels, local(): pl.pallas_call(functools.partial(faces_kernel, writers, capacity, region...  4.63 us

profile of v1, /device:TPU:0, one launch (start us, length us, event | category | flops | bytes accessed | tf_op | source)
XLA Modules:
  0.0 165.7 jit_solution(5354368850946655730)
XLA Ops:
  0.0 0.0 copy-start.2
  0.0 0.0 copy-start
  0.0 4.6 %faces.1 = (s32[16,128]{1,0:T(8,128)}, s32[16,128]{1,0:T(8,128)}, s32[32,128]{1,0:T(8,128)}, f32[2,2,32,128]{3,2,1,0:T(8,128)}, f32[2,2,64,128]{3,2,1,0:T(8,128)}, /*index=5*/f32[8,128]{1,0:T(8,128)}) custom-call(s32[16,128]{1,0:T(8,128)} %bitcast.44, s32[16,128]{1,0:T(8,128)} %bitcast.45, f32[3,32,64,128]{3,2,1,0:T(8,128)} %vel.5), custom_call_target="tpu_custom_call" | custom-call | tf_op jit(solution)/shard_map/faces/pallas_call | solution.py:390
  4.6 15.1 %halo.1 = (f32[6,2,64,128]{3,2,1,0:T(8,128)}, s32[1]{0:T(128)}) custom-call(f32[3,32,64,128]{3,2,1,0:T(8,128)} %vel.5, f32[2,2,32,128]{3,2,1,0:T(8,128)} %get-tuple-element.140.y_faces, f32[2,2,64,128]{3,2,1,0:T(8,128)} %get-tuple-element.141.z_faces, f32[8,128]{1,0:T(8,128)} %get-tuple-element.142.need), custom_call_target="tpu_custom_call" | custom-call | tf_op jit(solution)/shard_map/halo/pallas_call | solution.py:402
  20.4 0.0 copy-done.2
  20.4 0.0 copy-done
  20.4 0.0 copy-start.1
  20.4 1.0 copy-done.1
  21.4 0.0 copy-start.3
  21.4 0.7 copy-done.3
  22.1 0.0 copy-start.4
  22.1 0.7 copy-done.4
  22.8 0.0 copy-start.5
  22.8 0.7 copy-done.5
  23.5 22.0 %blocks.1 = (f32[12480,128]{1,0:T(8,128)}, f32[8,128]{1,0:T(8,128)S(1)}, s32[4096]{0:T(1024)S(1)}) custom-call(s32[2048]{0:T(1024)S(1)} %bitcast.18, s32[2048]{0:T(1024)S(1)} %bitcast.19, s32[4096]{0:T(1024)S(1)} %bitcast.17, f32[3,32,64,128]{3,2,1,0:T(8,128)S(1)} %copy-done, f32[6,2,64,128]{3,2,1,0:T(8,128)S(1)} %copy-done.1, bf16[256,256]{1,0:T(8,128)(2,1)S(1)} %copy-done.2), custom_call_target="tpu_custom_call" | custom-call | tf_op jit(solution)/shard_map/blocks/pallas_call | solution.py:424
  45.5 88.2 %conditional.1 = (f32[8,1560,128]{2,1,0:T(8,128)}, f32[8,128]{1,0:T(8,128)S(1)}, s32[4096]{0:T(1024)S(1)}) conditional(s32[]{:T(128)} %bitcast.10, (f32[8,1560,128]{2,1,0:T(8,128)}, f32[8,128]{1,0:T(8,128)S(1)}, s32[8,4,128]{2,1,0:T(4,128)S(1)}) %tuple.62, (f32[8,1560,128]{2,1,0:T(8,128)}, f32[8,128]{1,0:T(8,128)S(1)}, ...), branch_computations={%region_0.0_spmd, %region_1.0_spmd, %region_2.0_spmd, %region_3.0_... | conditional | bytes 24 | solution.py:475
  45.6 88.2 %exchange304.1 = (f32[8,1560,128]{2,1,0:T(8,128)}, f32[8,128]{1,0:T(8,128)S(1)}, s32[8,4,128]{2,1,0:T(4,128)S(1)}) custom-call(f32[8,1560,128]{2,1,0:T(8,128)} %get-tuple-element.90.send, f32[8,128]{1,0:T(8,128)S(1)} %get-tuple-element.91.squares, s32[8,4,128]{2,1,0:T(4,128)S(1)} %get-tuple-element.92.meta), custom_call_target="tpu_custom_call" | custom-call | tf_op jit(solution)/shard_map/cond/branch_2_fun/exchange304/pallas_call | solution.py:450
  133.7 32.0 %unpack.1 = f32[3,8,512,128]{3,2,1,0:T(8,128)} custom-call(s32[4096]{0:T(1024)S(1)} %get-tuple-element.151.meta, f32[8,128]{1,0:T(8,128)S(1)} %get-tuple-element.152.squares, f32[8,1560,128]{2,1,0:T(8,128)} %get-tuple-element.153.recv), custom_call_target="tpu_custom_call" | custom-call | tf_op jit(solution)/shard_map/unpack/pallas_call | solution.py:478
Async XLA Ops:
  0.0 20.4 %copy-start.2 = (bf16[256,256]{1,0:T(8,128)(2,1)S(1)}, bf16[256,256]{1,0:T(8,128)(2,1)}, u32[]{:S(2)}) copy-start(bf16[256,256]{1,0:T(8,128)(2,1)} %constant.8.clone.table) | copy-start | bytes 393220
  0.0 20.4 %copy-start = (f32[3,32,64,128]{3,2,1,0:T(8,128)S(1)}, f32[3,32,64,128]{3,2,1,0:T(8,128)}, u32[]{:S(2)}) copy-start(f32[3,32,64,128]{3,2,1,0:T(8,128)} %vel.5) | copy-start | bytes 9437188
  20.4 1.0 copy-start.1
  21.4 0.7 copy-start.3
  22.1 0.7 copy-start.4
  22.8 0.7 copy-start.5

commit v2 on v1

--- a/solution.py
+++ b/solution.py
@@ -1,4 +1,5 @@
 import functools
+import math
 
 import jax
 import jax.numpy as jnp
@@ -28,7 +29,7 @@
 
 
 def faces_kernel(
-    writers, capacity, pitch, targets, lens, vel, words, spots, blank, y_faces, z_faces, need
+    writers, capacity, region, targets, lens, vel, plan, y_faces, z_faces, need
 ):
     comps, cells_x, cells_y, cells_z = vel.shape
     lane = lax.broadcasted_iota(jnp.int32, (cells_y, cells_z), 1)
@@ -64,7 +65,7 @@
     weight = kept.astype(jnp.float32)
 
     def body(w, acc):
-        spot, start, most = acc
+        spot, start, site = acc
         mine = t == w
         ones = mine.astype(jnp.float32)
         sizes = jnp.where(mine, weight, 0.0)
@@ -75,21 +76,20 @@
         rank = inner[:rows] + jnp.sum(before[:, :lanes], axis=1, keepdims=True)
         offset = inner[rows:] + jnp.sum(before[:, lanes:], axis=1, keepdims=True)
         spot = jnp.where(mine, w * capacity + rank.astype(jnp.int32), spot)
-        start = jnp.where(mine, w * pitch + offset.astype(jnp.int32), start)
-        most = jnp.where(mine, offset + weight, most)
-        return spot, start, most
+        offset = offset.astype(jnp.int32)
+        start = jnp.where(mine, offset, start)
+        site = jnp.where(mine, w * region, site)
+        return spot, start, site
 
     none = jnp.zeros_like(t)
-    spot, start, most = lax.fori_loop(
-        0, writers, body, (none, none, jnp.zeros(t.shape, jnp.float32)), unroll=8
-    )
-    spots[...] = spot
-    words[...] = start * 256 + kept
+    spot, start, site = lax.fori_loop(0, writers, body, (none, none, none), unroll=8)
+    shift = start & (lanes - 1)
+    row = lax.shift_right_logical(start, lanes.bit_length() - 1)
+    plan[2] = spot
+    plan[0] = (row + site) * (comps << 16) + shift
+    plan[1] = row * (comps << 16) + (lanes - shift) * 256 + kept
+    most = (start + kept).astype(jnp.float32)
     need[...] = jnp.max(most.reshape(rows // 8, 8, lanes), axis=0)
-    place = lax.broadcasted_iota(jnp.int32, blank.shape, 0) * lanes + lax.broadcasted_iota(
-        jnp.int32, blank.shape, 1
-    )
-    blank[...] = lax.div(place, capacity) * (pitch * 256)
 
 
 def plane_peers(n_x, n_y):
@@ -184,7 +184,9 @@
     return tiles.reshape(cells_y, cells_z)
 
 
-def blocks_kernel(words, spots, blank, vel, halos, table, out, squares, meta, coeffs, meta_sem):
+def blocks_kernel(
+    lists, blank, vel, halos, table, out, squares, meta, coeffs, plan, meta_sem, plan_sem
+):
     comps, cells_x, cells_y, cells_z = vel.shape
     nblk = coeffs.shape[0] // comps
     per_plane = nblk // cells_x
@@ -193,6 +195,8 @@
     lane = lax.broadcasted_iota(jnp.int32, (cells_y, cells_z), 1)
     clear = pltpu.make_async_copy(blank, meta, meta_sem)
     clear.start()
+    fetch = pltpu.make_async_copy(lists, plan, plan_sem)
+    fetch.start()
 
     def plane(x, acc):
         u, v, w = vel[0, x], vel[1, x], vel[2, x]
@@ -247,10 +251,10 @@
             found = []
             for k in range(start, min(start + group, per_plane)):
                 i = x * per_plane + k
-                word = words[i]
-                meta[spots[i]] = word
-                shift = lax.shift_right_logical(word, 8) & (width - 1)
-                row = lax.shift_right_logical(word, 15) * comps
+                word = plan[i]
+                meta[plan[2 * nblk + i]] = plan[nblk + i]
+                shift = word & (width - 1)
+                row = lax.shift_right_logical(word, 16)
                 moved = pltpu.roll(coeffs[pl.ds(i * comps, comps), :], shift, 1)
                 found.append((row, moved, spread >= shift))
             for row, moved, mask in found:
@@ -270,6 +274,7 @@
         return acc
 
     clear.wait()
+    fetch.wait()
     first = planes(0, jnp.zeros((8, cells_z), jnp.float32))
     squares[...] = lax.fori_loop(1, cells_x // together, step, first)
     for k in range(together):
@@ -331,10 +336,9 @@
     total[...] = jnp.sum(near[...], axis=0) + jnp.sum(far[...], axis=(0, 1))
 
 
-def unpack_kernel(every, n_y, pitch, meta, squares, recv, out, scale):
+def unpack_kernel(every, meta, squares, recv, out, scale):
     comps, _, capacity, width = out.shape
     source = pl.program_id(0)
-    base = (lax.axis_index("gx") * n_y + lax.axis_index("gy")) * pitch
 
     @pl.when(source == 0)
     def _():
@@ -343,24 +347,23 @@
 
     lane = lax.broadcasted_iota(jnp.int32, (comps, width), 1)
     factor = scale[:comps]
-    group = 16 if capacity % 16 == 0 else 8
+    group = math.gcd(capacity, 32)
+    first = source * capacity
 
     def some(t, _):
-        found = []
+        start = first + t * group
         for k in range(group):
-            slot = t * group + k
-            word = meta[source * capacity + slot]
-            length = word & 255
-            shift = lax.shift_right_logical(word, 8) & (width - 1)
-            row = (lax.shift_right_logical(word, 15) - base) * comps
+            mark = meta[start + k]
+            fields = jnp.full((comps, width), mark, jnp.int32)
+            ahead = lane + (lax.shift_right_logical(fields, 8) & 255)
+            row = lax.shift_right_logical(mark, 16)
             head = recv[0, pl.ds(row, comps), :]
             tail = recv[0, pl.ds(row + comps, comps), :]
-            joined = jnp.where(lane >= shift, head, tail)
-            moved = pltpu.roll(joined, (width - shift) & (width - 1), 1)
-            found.append((slot, jnp.where(lane < length, moved * factor, 0.0)))
-        for slot, value in found:
+            joined = jnp.where(ahead >= width, head, tail)
+            moved = pltpu.roll(joined, lax.shift_right_logical(mark, 8) & (width - 1), 1)
+            value = jnp.where(lane < (fields & 255), moved * factor, 0.0)
             for c in range(comps):
-                out[c, 0, pl.ds(slot, 1), :] = value[c : c + 1]
+                out[c, 0, pl.ds(t * group + k, 1), :] = value[c : c + 1]
         return 0
 
     lax.fori_loop(0, capacity // group, some, 0)
@@ -386,13 +389,10 @@
     vmem = pl.BlockSpec(memory_space=pltpu.VMEM)
     anywhere = pl.BlockSpec(memory_space=pl.ANY)
     dma = pltpu.SemaphoreType.DMA
-    flat = jax.ShapeDtypeStruct((nblk // 128, 128), jnp.int32)
-    words, spots, blank, y_faces, z_faces, need = pl.pallas_call(
-        functools.partial(faces_kernel, writers, capacity, region * width),
+    plan, y_faces, z_faces, need = pl.pallas_call(
+        functools.partial(faces_kernel, writers, capacity, region),
         out_shape=(
-            flat,
-            flat,
-            jax.ShapeDtypeStruct((writers * capacity // 128, 128), jnp.int32),
+            jax.ShapeDtypeStruct((3, nblk // 128, 128), jnp.int32),
             jax.ShapeDtypeStruct((2, 2, cells_x, cells_z), f32),
             jax.ShapeDtypeStruct((2, 2, cells_y, cells_z), f32),
             jax.ShapeDtypeStruct((8, 128), f32),
@@ -428,15 +428,19 @@
             jax.ShapeDtypeStruct((8, cells_z), f32),
             jax.ShapeDtypeStruct((writers * capacity,), jnp.int32),
         ),
-        in_specs=[smem, smem] + [anywhere] + [vmem] * 3,
+        in_specs=[anywhere] * 2 + [vmem] * 3,
         out_specs=(vmem, vmem, smem),
-        scratch_shapes=[pltpu.VMEM((nblk * comps, width), f32), dma],
+        scratch_shapes=[
+            pltpu.VMEM((nblk * comps, width), f32),
+            pltpu.SMEM((3 * nblk,), jnp.int32),
+            dma,
+            dma,
+        ],
         compiler_params=pltpu.CompilerParams(vmem_limit_bytes=48 * 2**20),
         name="blocks",
     )(
-        words.reshape(nblk),
-        spots.reshape(nblk),
-        blank.reshape(writers * capacity),
+        plan.reshape(3 * nblk),
+        jnp.zeros((writers * capacity,), jnp.int32),
         velocity,
         halos,
         table,
@@ -476,7 +480,7 @@
 
     every = velocity.size * n_x * n_y * n_z
     received = pl.pallas_call(
-        functools.partial(unpack_kernel, float(every), n_y, region),
+        functools.partial(unpack_kernel, float(every)),
         grid=(writers,),
         in_specs=[
             smem,

time: 166 us -> 148 us (0.89)
  Pallas kernels: 162 us -> 145 us
    pallas_call x2, Pallas kernels: 36.6 us -> 23.7 us  [the longest x1 19 us: local(): pl.pallas_call(functools.partial(unpack_kernel, float(every)), grid=(writ...]
    pallas_call x1, Pallas kernels: 22 us -> 18 us  [local(): pl.pallas_call(blocks_kernel, out_shape=(jax.ShapeDtypeStruct((writers *...]
where the time goes in v2:
time: 148 us; the launch traced here: 147 us
  Pallas kernels  145 us (98%)
  local copies, waits for them, and re-layouts  1.74 us (1%)
    pallas_call x1, Pallas kernels, exchange(): pl.pallas_call(functools.partial(exchange_kernel, n_x, n_y, n_z, rows), o...  88.2 us
    pallas_call x1, Pallas kernels, local(): pl.pallas_call(functools.partial(unpack_kernel, float(every)), grid=(writ...  19 us
    pallas_call x1, Pallas kernels, local(): pl.pallas_call(blocks_kernel, out_shape=(jax.ShapeDtypeStruct((writers *...  18 us
    pallas_call x1, Pallas kernels, local(): pl.pallas_call(functools.partial(halo_kernel, (n_x, n_y, n_z), tiers), ou...  15.1 us
    pallas_call x1, Pallas kernels, local(): pl.pallas_call(functools.partial(faces_kernel, writers, capacity, region)...  4.63 us

profile of v2, /device:TPU:0, one launch (start us, length us, event | category | flops | bytes accessed | tf_op | source)
XLA Modules:
  0.0 147.4 jit_solution(5971683633769547612)
XLA Ops:
  0.0 0.0 copy-start.2
  0.0 0.0 copy-start
  0.0 4.6 %faces.1 = (s32[3,16,128]{2,1,0:T(8,128)}, f32[2,2,32,128]{3,2,1,0:T(8,128)}, f32[2,2,64,128]{3,2,1,0:T(8,128)}, f32[8,128]{1,0:T(8,128)}) custom-call(s32[16,128]{1,0:T(8,128)} %bitcast.40, s32[16,128]{1,0:T(8,128)} %bitcast.41, f32[3,32,64,128]{3,2,1,0:T(8,128)} %vel.5), custom_call_target="tpu_custom_call" | custom-call | tf_op jit(solution)/shard_map/faces/pallas_call | solution.py:392
  4.6 15.1 %halo.1 = (f32[6,2,64,128]{3,2,1,0:T(8,128)}, s32[1]{0:T(128)}) custom-call(f32[3,32,64,128]{3,2,1,0:T(8,128)} %vel.5, f32[2,2,32,128]{3,2,1,0:T(8,128)} %get-tuple-element.138.y_faces, f32[2,2,64,128]{3,2,1,0:T(8,128)} %get-tuple-element.139.z_faces, f32[8,128]{1,0:T(8,128)} %get-tuple-element.140.need), custom_call_target="tpu_custom_call" | custom-call | tf_op jit(solution)/shard_map/halo/pallas_call | solution.py:402
  20.4 0.0 copy-done.2
  20.4 0.0 copy-done
  20.4 0.0 copy-start.1
  20.4 1.0 copy-done.1
  21.4 0.0 copy-start.3
  21.4 0.7 copy-done.3
  22.2 18.0 %blocks.1 = (f32[12480,128]{1,0:T(8,128)}, f32[8,128]{1,0:T(8,128)S(1)}, s32[4096]{0:T(1024)S(1)}) custom-call(s32[6144]{0:T(1024)S(1)} %bitcast.15, s32[4096]{0:T(1024)S(1)} %broadcast_in_dim.3.blank, f32[3,32,64,128]{3,2,1,0:T(8,128)S(1)} %copy-done, f32[6,2,64,128]{3,2,1,0:T(8,128)S(1)} %copy-done.1, bf16[256,256]{1,0:T(8,128)(2,1)S(1)} %copy-done.2), custom_call_target="tpu_custom_call" | custom-call | tf_op jit(solution)/shard_map/blocks/pallas_call | solution.py:424
  40.1 88.2 %conditional.1 = (f32[8,1560,128]{2,1,0:T(8,128)}, f32[8,128]{1,0:T(8,128)S(1)}, s32[4096]{0:T(1024)S(1)}) conditional(s32[]{:T(128)} %bitcast.10, (f32[8,1560,128]{2,1,0:T(8,128)}, f32[8,128]{1,0:T(8,128)S(1)}, s32[8,4,128]{2,1,0:T(4,128)S(1)}) %tuple.62, (f32[8,1560,128]{2,1,0:T(8,128)}, f32[8,128]{1,0:T(8,128)S(1)}, ...), branch_computations={%region_0.0_spmd, %region_1.0_spmd, %region_2.0_spmd, %region_3.0_... | conditional | bytes 24 | solution.py:479
  40.2 88.2 %exchange304.1 = (f32[8,1560,128]{2,1,0:T(8,128)}, f32[8,128]{1,0:T(8,128)S(1)}, s32[8,4,128]{2,1,0:T(4,128)S(1)}) custom-call(f32[8,1560,128]{2,1,0:T(8,128)} %get-tuple-element.90.send, f32[8,128]{1,0:T(8,128)S(1)} %get-tuple-element.91.squares, s32[8,4,128]{2,1,0:T(4,128)S(1)} %get-tuple-element.92.meta), custom_call_target="tpu_custom_call" | custom-call | tf_op jit(solution)/shard_map/cond/branch_2_fun/exchange304/pallas_call | solution.py:454
  128.4 19.0 %unpack.1 = f32[3,8,512,128]{3,2,1,0:T(8,128)} custom-call(s32[4096]{0:T(1024)S(1)} %get-tuple-element.147.meta, f32[8,128]{1,0:T(8,128)S(1)} %get-tuple-element.148.squares, f32[8,1560,128]{2,1,0:T(8,128)} %get-tuple-element.149.recv), custom_call_target="tpu_custom_call" | custom-call | tf_op jit(solution)/shard_map/unpack/pallas_call | solution.py:482
  (1 shorter events, 0.0 us)
Async XLA Ops:
  0.0 20.4 %copy-start.2 = (bf16[256,256]{1,0:T(8,128)(2,1)S(1)}, bf16[256,256]{1,0:T(8,128)(2,1)}, u32[]{:S(2)}) copy-start(bf16[256,256]{1,0:T(8,128)(2,1)} %constant.10.clone.table) | copy-start | bytes 393220
  0.0 20.4 %copy-start = (f32[3,32,64,128]{3,2,1,0:T(8,128)S(1)}, f32[3,32,64,128]{3,2,1,0:T(8,128)}, u32[]{:S(2)}) copy-start(f32[3,32,64,128]{3,2,1,0:T(8,128)} %vel.5) | copy-start | bytes 9437188
  20.4 1.0 copy-start.1
  21.4 0.7 copy-start.3

commit v3 on v2

--- a/solution.py
+++ b/solution.py
@@ -28,8 +28,13 @@
     return np.block([[high, low], [high, np.zeros_like(low)]]).astype(jnp.bfloat16)
 
 
+def spill_tiles(used, direct):
+    return lax.shift_right_logical(jnp.maximum(used - direct, 0) + 7, 3)
+
+
 def faces_kernel(
-    writers, capacity, region, targets, lens, vel, plan, y_faces, z_faces, need
+    writers, capacity, region, direct, n_y, targets, lens, vel, plan, counts, y_faces, z_faces, need,
+    sums
 ):
     comps, cells_x, cells_y, cells_z = vel.shape
     lane = lax.broadcasted_iota(jnp.int32, (cells_y, cells_z), 1)
@@ -70,6 +75,7 @@
         ones = mine.astype(jnp.float32)
         sizes = jnp.where(mine, weight, 0.0)
         both = jnp.concatenate([ones, sizes], axis=0).astype(jnp.bfloat16)
+        sums[pl.ds(w, 1), :] = jnp.sum(sizes, axis=0, keepdims=True)
         inner = jnp.dot(both, upper, preferred_element_type=jnp.float32)
         side = jnp.concatenate([ones, sizes], axis=1).astype(jnp.bfloat16)
         before = jnp.dot(lower, side, preferred_element_type=jnp.float32)
@@ -88,15 +94,27 @@
     plan[2] = spot
     plan[0] = (row + site) * (comps << 16) + shift
     plan[1] = row * (comps << 16) + (lanes - shift) * 256 + kept
-    most = (start + kept).astype(jnp.float32)
-    need[...] = jnp.max(most.reshape(rows // 8, 8, lanes), axis=0)
+    used = jnp.sum(sums[...], axis=1, keepdims=True).astype(jnp.int32)
+    used = jnp.broadcast_to(lax.shift_right_logical(used + (lanes - 1), 7), counts.shape)
+    counts[...] = used
+    writer = lax.broadcasted_iota(jnp.int32, counts.shape, 0)
+    half = max(1, n_y // 2)
+    far_side = lax.div(lax.rem(writer, n_y), half) != lax.div(lax.axis_index("gy"), half)
+    over = jnp.where(far_side, spill_tiles(used, direct) * 8, 0)
+    most = jnp.max(used.astype(jnp.float32), axis=0, keepdims=True)
+    extra = jnp.sum(over.astype(jnp.float32), axis=0, keepdims=True)
+    line = lax.broadcasted_iota(jnp.int32, need.shape, 0)
+    need[...] = jnp.where(line == 0, most, jnp.where(line == 1, extra, 0.0))
+
+
+def plane_offsets(n_x, n_y):
+    offsets = [(i, j) for i in range(n_x) for j in range(n_y) if i or j]
+    return sorted(offsets, key=lambda o: (bool(o[0]) and bool(o[1]), min(o[1], n_y - o[1])))
 
 
 def plane_peers(n_x, n_y):
     a, b, c = (lax.axis_index(axis) for axis in ("gx", "gy", "wa"))
-    offsets = [(i, j) for i in range(n_x) for j in range(n_y) if i or j]
-    offsets.sort(key=lambda o: (bool(o[0]) and bool(o[1]), min(o[1], n_y - o[1])))
-    return [(lax.rem(a + i, n_x), lax.rem(b + j, n_y), c) for i, j in offsets]
+    return [(lax.rem(a + i, n_x), lax.rem(b + j, n_y), c) for i, j in plane_offsets(n_x, n_y)]
 
 
 def line_mates(n_z):
@@ -165,8 +183,15 @@
     for copy in copies:
         copy.wait()
     most = jnp.maximum(jnp.max(near[...], axis=0), jnp.max(far[...], axis=(0, 1)))
-    above = jnp.max(most)
-    tier[0] = sum((above > 128.0 * rows).astype(jnp.int32) for rows in tiers[:-1])
+    pair, extra = jnp.max(most[0:1]), jnp.max(most[1:2])
+    chosen = jnp.int32(len(tiers) - 1)
+    for index in reversed(range(len(tiers) - 1)):
+        rows, spill = tiers[index]
+        fits = pair <= rows
+        if spill:
+            fits = jnp.logical_and(fits, extra <= spill)
+        chosen = jnp.where(fits, index, chosen)
+    tier[0] = chosen
 
 
 def block_rows(plane):
@@ -185,7 +210,8 @@
 
 
 def blocks_kernel(
-    lists, blank, vel, halos, table, out, squares, meta, coeffs, plan, meta_sem, plan_sem
+    n_x, n_y, region, direct, lists, tallies, blank, vel, halos, table, out, squares, meta, spill,
+    starts, coeffs, plan, counts, meta_sem, plan_sem, count_sem,
 ):
     comps, cells_x, cells_y, cells_z = vel.shape
     nblk = coeffs.shape[0] // comps
@@ -197,6 +223,8 @@
     clear.start()
     fetch = pltpu.make_async_copy(lists, plan, plan_sem)
     fetch.start()
+    tally = pltpu.make_async_copy(tallies, counts, count_sem)
+    tally.start()
 
     def plane(x, acc):
         u, v, w = vel[0, x], vel[1, x], vel[2, x]
@@ -275,33 +303,73 @@
 
     clear.wait()
     fetch.wait()
+    tally.wait()
     first = planes(0, jnp.zeros((8, cells_z), jnp.float32))
     squares[...] = lax.fori_loop(1, cells_x // together, step, first)
     for k in range(together):
         place(cells_x - together + k)
 
+    half = max(1, n_y // 2)
+    facing = lax.rem(lax.div(lax.axis_index("gy"), half) + 1, 2) * half
+    most = spill.shape[0] // comps
+
+    def segment(j, begin):
+        writer = lax.div(j, half) * n_y + facing + lax.rem(j, half)
+        tiles = jnp.minimum(spill_tiles(counts[writer, 0], direct), most - begin)
+        starts[j] = begin
+        source = (writer * region + direct) * comps
+
+        def tile(i, _):
+            for c in range(comps):
+                at = source + (i * comps + c) * 8
+                spill[(begin + i) * comps + c] = out[pl.ds(pl.multiple_of(at, 8), 8), :]
+            return 0
+
+        lax.fori_loop(0, tiles, tile, 0)
+        return begin + tiles
+
+    lax.fori_loop(0, n_x * half, segment, jnp.int32(0))
+
 
 def exchange_kernel(
-    n_x, n_y, n_z, rows, send, squares, meta, recv, total, heard, near, far, send_sem, recv_sem,
-    part_send, part_recv, word_send, word_recv, own_sem,
+    n_x, n_y, n_z, comps, rows, direct, extra, send, squares, meta, spill, starts, recv, total, heard,
+    near, far, send_sem, recv_sem, part_send, part_recv, word_send, word_recv, own_sem, *relay,
 ):
     a, b = lax.axis_index("gx"), lax.axis_index("gy")
     c = lax.axis_index("wa")
     me = a * n_y + b
+    half = max(1, n_y // 2)
     peers, mates = plane_peers(n_x, n_y), line_mates(n_z)
     barrier = pltpu.get_barrier_semaphore()
     for device in mates + peers:
         pl.semaphore_signal(barrier, inc=1, device_id=device, device_id_type=MESH)
     pl.semaphore_wait(barrier, len(peers) + len(mates))
-    used = pl.ds(0, rows)
 
     own = [
         pltpu.make_async_copy(squares, near.at[c], own_sem.at[0]),
         pltpu.make_async_copy(meta.at[me], heard.at[me], own_sem.at[1]),
-        pltpu.make_async_copy(send.at[me, used], recv.at[me, used], own_sem.at[2]),
+        pltpu.make_async_copy(
+            send.at[me, pl.ds(0, rows * comps)], recv.at[me, pl.ds(0, rows * comps)], own_sem.at[2]
+        ),
     ]
     for copy in own:
         copy.start()
+    copies, relays = [], []
+    if extra:
+        (
+            landed, ready, begins, marks, relay_send, relay_recv, spill_send, spill_recv, begin_sem
+        ) = relay
+        partner = (a, lax.rem(b + half, n_y), c)
+        relays = [
+            send_to(starts, begins, spill_send.at[0], spill_recv.at[0], partner),
+            send_to(
+                spill.at[pl.ds(0, extra * comps // 8)],
+                landed.at[pl.ds(0, extra * comps // 8)],
+                spill_send.at[1],
+                spill_recv.at[1],
+                partner,
+            ),
+        ]
     first = [
         send_to(squares, near.at[c], part_send.at[k], part_recv.at[k], device)
         for k, device in enumerate(mates)
@@ -310,29 +378,108 @@
     def number(device):
         return device[0] * n_y + device[1]
 
+    offsets = plane_offsets(n_x, n_y)
+
     def blocks_to(k):
         device = peers[k]
-        return send_to(
-            send.at[number(device), used], recv.at[me, used], send_sem.at[k], recv_sem.at[k], device
+
+        def go(size):
+            used = pl.ds(0, size * comps)
+            return pltpu.make_async_remote_copy(
+                src_ref=send.at[number(device), used],
+                dst_ref=recv.at[me, used],
+                send_sem=send_sem.at[k],
+                recv_sem=recv_sem.at[k],
+                device_id=device,
+                device_id_type=MESH,
+            )
+
+        if not extra:
+            copy = go(rows)
+            copy.start()
+            return [copy.wait]
+        crosses = lax.div(device[1], half) != lax.div(b, half)
+        inward = lax.div(lax.rem(b - offsets[k][1] + n_y, n_y), half) != lax.div(b, half)
+
+        @pl.when(crosses)
+        def _():
+            go(direct).start()
+
+        @pl.when(jnp.logical_not(crosses))
+        def _():
+            go(rows).start()
+
+        def wait():
+            @pl.when(crosses)
+            def _():
+                go(direct).wait_send()
+
+            @pl.when(jnp.logical_not(crosses))
+            def _():
+                go(rows).wait_send()
+
+            @pl.when(inward)
+            def _():
+                go(direct).wait_recv()
+
+            @pl.when(jnp.logical_not(inward))
+            def _():
+                go(rows).wait_recv()
+
+        return [wait]
+
+    waits = []
+    for k, device in enumerate(peers):
+        copies.append(
+            send_to(meta.at[number(device)], heard.at[me], word_send.at[k], word_recv.at[k], device)
         )
-
-    copies = [
-        send_to(meta.at[number(device)], heard.at[me], word_send.at[k], word_recv.at[k], device)
-        for k, device in enumerate(peers)
-    ]
     ahead = min(3, len(peers))
-    copies += [blocks_to(k) for k in range(ahead)]
+    for k in range(ahead):
+        waits += blocks_to(k)
     own[0].wait()
     for copy in first:
         copy.wait()
     for k, device in enumerate(peers):
         sem = n_z - 1 + k
         copies.append(send_to(near, far.at[k], part_send.at[sem], part_recv.at[sem], device))
-    copies += [blocks_to(k) for k in range(ahead, len(peers))]
+    for k in range(ahead, len(peers)):
+        waits += blocks_to(k)
+    if extra:
+        relays[0].wait()
+        load = pltpu.make_async_copy(begins, marks, begin_sem.at[0])
+        load.start()
+        load.wait()
+        relays[1].wait()
+        size = (rows - direct) * comps
+        source = a * n_y + lax.rem(b + half, n_y)
+        mine = lax.rem(b, half)
+        base = b - mine
+        places = [
+            (lax.rem(a + i, n_x), lax.rem(mine + j, half)) for i in range(n_x) for j in range(half)
+        ]
+        for k, (x, y) in enumerate(places):
+            begin = marks[0, x * half + y] * comps
+
+            def tile(i, _, k=k, begin=begin):
+                ready[k, pl.ds(pl.multiple_of(i * 8, 8), 8), :] = landed[begin + i]
+                return 0
+
+            lax.fori_loop(0, size // 8, tile, 0)
+        spot = recv.at[source, pl.ds(direct * comps, size)]
+        for k, (x, y) in enumerate(places):
+            if k:
+                copies.append(
+                    send_to(ready.at[k], spot, relay_send.at[k], relay_recv.at[k], (x, base + y, c))
+                )
+        keep = pltpu.make_async_copy(ready.at[0], spot, begin_sem.at[1])
+        keep.start()
+        keep.wait()
     for copy in own[1:]:
         copy.wait()
     for copy in copies:
         copy.wait()
+    for wait in waits:
+        wait()
     total[...] = jnp.sum(near[...], axis=0) + jnp.sum(far[...], axis=(0, 1))
 
 
@@ -369,9 +516,16 @@
     lax.fori_loop(0, capacity // group, some, 0)
 
 
-def tier_rows(capacity):
-    steps = (16, 18, 19, 20, 22, 24, 28, 32)
-    return sorted({-(-capacity * step // (32 * 8)) * 8 for step in steps})
+def tier_sizes(capacity, n_y):
+    def up(part):
+        return -(-capacity * part // (64 * 8)) * 8
+
+    direct = [(up(part), 0) for part in (48, 56, 64)]
+    if n_y % 2:
+        return up(64), direct
+    parts = ((38, 28), (38, 32), (39, 36), (40, 44), (44, 52))
+    spilled = [(up(rows), up(extra)) for rows, extra in parts]
+    return up(18), spilled + direct
 
 
 def local(velocity, lengths, destinations):
@@ -383,20 +537,24 @@
     capacity = max(2, 2 * nblk // writers)
     region = capacity + 8
     f32 = jnp.float32
-    tiers = tier_rows(capacity)
+    direct, tiers = tier_sizes(capacity, n_y)
+    most_extra = max([8] + [extra for _, extra in tiers])
+    senders = n_x * max(1, n_y // 2)
 
     smem = pl.BlockSpec(memory_space=pltpu.SMEM)
     vmem = pl.BlockSpec(memory_space=pltpu.VMEM)
     anywhere = pl.BlockSpec(memory_space=pl.ANY)
     dma = pltpu.SemaphoreType.DMA
-    plan, y_faces, z_faces, need = pl.pallas_call(
-        functools.partial(faces_kernel, writers, capacity, region),
+    plan, tallies, y_faces, z_faces, need = pl.pallas_call(
+        functools.partial(faces_kernel, writers, capacity, region, direct, n_y),
         out_shape=(
             jax.ShapeDtypeStruct((3, nblk // 128, 128), jnp.int32),
+            jax.ShapeDtypeStruct((writers, 128), jnp.int32),
             jax.ShapeDtypeStruct((2, 2, cells_x, cells_z), f32),
             jax.ShapeDtypeStruct((2, 2, cells_y, cells_z), f32),
             jax.ShapeDtypeStruct((8, 128), f32),
         ),
+        scratch_shapes=[pltpu.VMEM((writers, 128), f32)],
         name="faces",
     )(destinations.reshape(nblk // 128, 128), lengths.reshape(nblk // 128, 128), velocity)
     halos, tier = pl.pallas_call(
@@ -421,18 +579,22 @@
     )(velocity, y_faces, z_faces, need)
 
     table = jnp.asarray(split_table())
-    outgoing, squares, meta = pl.pallas_call(
-        blocks_kernel,
+    outgoing, squares, meta, spill, starts = pl.pallas_call(
+        functools.partial(blocks_kernel, n_x, n_y, region, direct),
         out_shape=(
             jax.ShapeDtypeStruct((writers * region * comps, width), f32),
             jax.ShapeDtypeStruct((8, cells_z), f32),
             jax.ShapeDtypeStruct((writers * capacity,), jnp.int32),
+            jax.ShapeDtypeStruct((most_extra * comps // 8, 8, width), f32),
+            jax.ShapeDtypeStruct((128,), jnp.int32),
         ),
-        in_specs=[anywhere] * 2 + [vmem] * 3,
-        out_specs=(vmem, vmem, smem),
+        in_specs=[anywhere] * 3 + [vmem] * 3,
+        out_specs=(vmem, vmem, smem, vmem, smem),
         scratch_shapes=[
             pltpu.VMEM((nblk * comps, width), f32),
             pltpu.SMEM((3 * nblk,), jnp.int32),
+            pltpu.SMEM((writers, 128), jnp.int32),
+            dma,
             dma,
             dma,
         ],
@@ -440,6 +602,7 @@
         name="blocks",
     )(
         plan.reshape(3 * nblk),
+        tallies,
         jnp.zeros((writers * capacity,), jnp.int32),
         velocity,
         halos,
@@ -449,16 +612,28 @@
     part = min(capacity, 128)
     meta = meta.reshape(writers, capacity // part, part)
 
-    def exchange(index, outgoing, squares, meta):
-        rows = tiers[index] * comps
+    def exchange(index, *operands):
+        rows, extra = tiers[index]
+        size = (rows - direct) * comps
+        relay = [
+            pltpu.VMEM(((extra * comps + size) // 8, 8, width), f32),
+            pltpu.VMEM((senders, size, width), f32),
+            pltpu.VMEM((1, 128), jnp.int32),
+            pltpu.SMEM((1, 128), jnp.int32),
+            dma((senders,)),
+            dma((senders,)),
+            dma((2,)),
+            dma((2,)),
+            dma((2,)),
+        ]
         return pl.pallas_call(
-            functools.partial(exchange_kernel, n_x, n_y, n_z, rows),
+            functools.partial(exchange_kernel, n_x, n_y, n_z, comps, rows, direct, extra),
             out_shape=(
                 jax.ShapeDtypeStruct(outgoing.shape, f32),
                 jax.ShapeDtypeStruct(squares.shape, f32),
                 jax.ShapeDtypeStruct(meta.shape, jnp.int32),
             ),
-            in_specs=[anywhere, vmem, anywhere],
+            in_specs=[anywhere, vmem, anywhere, anywhere, anywhere],
             out_specs=(anywhere, vmem, anywhere),
             scratch_shapes=[
                 pltpu.VMEM((n_z,) + squares.shape, f32),
@@ -470,13 +645,16 @@
                 dma((writers - 1,)),
                 dma((writers - 1,)),
                 dma((3,)),
-            ],
+            ]
+            + (relay if extra else []),
             compiler_params=pltpu.CompilerParams(collective_id=2 + index, has_side_effects=True),
-            name=f"exchange{tiers[index]}",
-        )(outgoing, squares, meta)
+            name=f"exchange{rows}_{extra}",
+        )(*operands)
 
     branches = [functools.partial(exchange, index) for index in range(len(tiers))]
-    arrived, squares, heard = lax.switch(tier[0], branches, outgoing, squares, meta)
+    arrived, squares, heard = lax.switch(
+        tier[0], branches, outgoing, squares, meta, spill, starts.reshape(1, 128)
+    )
 
     every = velocity.size * n_x * n_y * n_z
     received = pl.pallas_call(

time: 148 us -> 130 us (0.88); the launches traced: 147 us -> 128 us
  Pallas kernels: 145 us -> 125 us
    pallas_call x3, Pallas kernels: 111 us -> 90.4 us  [the longest x1 67.2 us: exchange(): pl.pallas_call(functools.partial(exchange_kernel, n_x, n_y, n_z, comps, r...]
where the time goes in v3:
time: 130 us; the launch traced here: 128 us
  Pallas kernels  125 us (96%)
  local copies, waits for them, and re-layouts  2.41 us (2%)
    pallas_call x1, Pallas kernels, exchange(): pl.pallas_call(functools.partial(exchange_kernel, n_x, n_y, n_z, comps, r...  67.2 us
    pallas_call x1, Pallas kernels, local(): pl.pallas_call(functools.partial(unpack_kernel, float(every)), grid=(writ...  19 us
    pallas_call x1, Pallas kernels, local(): pl.pallas_call(functools.partial(blocks_kernel, n_x, n_y, region, direct)...  18.6 us
    pallas_call x1, Pallas kernels, local(): pl.pallas_call(functools.partial(halo_kernel, (n_x, n_y, n_z), tiers), ou...  15.1 us
    pallas_call x1, Pallas kernels, local(): pl.pallas_call(functools.partial(faces_kernel, writers, capacity, region,...  4.64 us

profile of v3, /device:TPU:0, one launch (start us, length us, event | category | flops | bytes accessed | tf_op | source)
XLA Modules:
  0.0 127.7 jit_solution(14540409194160455740)
XLA Ops:
  0.0 0.0 copy-start.2
  0.0 0.0 copy-start
  0.0 4.6 %faces.1 = (s32[3,16,128]{2,1,0:T(8,128)}, s32[8,128]{1,0:T(8,128)}, f32[2,2,32,128]{3,2,1,0:T(8,128)}, f32[2,2,64,128]{3,2,1,0:T(8,128)}, f32[8,128]{1,0:T(8,128)}) custom-call(s32[16,128]{1,0:T(8,128)} %bitcast.49, s32[16,128]{1,0:T(8,128)} %bitcast.50, f32[3,32,64,128]{3,2,1,0:T(8,128)} %vel.5), custom_call_target="tpu_custom_call" | custom-call | tf_op jit(solution)/shard_map/faces/pallas_call | solution.py:548
  4.6 15.1 %halo.1 = (f32[6,2,64,128]{3,2,1,0:T(8,128)}, s32[1]{0:T(128)}) custom-call(f32[3,32,64,128]{3,2,1,0:T(8,128)} %vel.5, f32[2,2,32,128]{3,2,1,0:T(8,128)} %get-tuple-element.189.y_faces, f32[2,2,64,128]{3,2,1,0:T(8,128)} %get-tuple-element.190.z_faces, f32[8,128]{1,0:T(8,128)} %get-tuple-element.191.need), custom_call_target="tpu_custom_call" | custom-call | tf_op jit(solution)/shard_map/halo/pallas_call | solution.py:560
  20.4 0.0 copy-done.2
  20.4 0.0 copy-done
  20.4 0.0 copy-start.1
  20.5 1.0 copy-done.1
  21.4 0.0 copy-start.3
  21.4 0.7 copy-done.3
  22.2 0.0 copy-start.4
  22.2 0.7 copy-done.4
  22.9 18.6 %blocks.1 = (f32[12480,128]{1,0:T(8,128)}, f32[8,128]{1,0:T(8,128)S(1)}, s32[4096]{0:T(1024)S(1)}, f32[156,8,128]{2,1,0:T(8,128)}, s32[128]{0:T(128)S(1)}) custom-call(s32[6144]{0:T(1024)S(1)} %bitcast.16, s32[8,128]{1,0:T(8,128)S(1)} %copy-done.4, s32[4096]{0:T(1024)S(1)} %broadcast_in_dim.3.blank, f32[3,32,64,128]{3,2,1,0:T(8,128)S(1)} %copy-done, ...), custom_call_target="tpu_custom_call" | custom-call | tf_op jit(solution)/shard_map/blocks/pallas_call | solution.py:582
  41.5 67.2 %conditional.1 = (f32[8,1560,128]{2,1,0:T(8,128)}, f32[8,128]{1,0:T(8,128)S(1)}, s32[4096]{0:T(1024)S(1)}) conditional(s32[]{:T(128)} %bitcast.10, (f32[8,1560,128]{2,1,0:T(8,128)}, f32[8,128]{1,0:T(8,128)S(1)}, s32[8,4,128]{2,1,0:T(4,128)S(1)}, f32[156,8,128]{2,1,0:T(8,128)}, s32[1,128]{1,0:T(1,128)S(1)}) %tuple.70, ...), branch_computations={%region_0.0_spmd, %region_1.0_spmd, %region_2.0_spmd, %region_3.0_... | conditional | bytes 24 | solution.py:655
  41.5 67.2 %exchange312_288.1 = (f32[8,1560,128]{2,1,0:T(8,128)}, f32[8,128]{1,0:T(8,128)S(1)}, s32[8,4,128]{2,1,0:T(4,128)S(1)}) custom-call(f32[8,1560,128]{2,1,0:T(8,128)} %get-tuple-element.126.send, f32[8,128]{1,0:T(8,128)S(1)} %get-tuple-element.127.squares, s32[8,4,128]{2,1,0:T(4,128)S(1)} %get-tuple-element.128.meta, f32[156,8,128]{2,1,0:T(8,128)} %get-tuple-element.129.spill, ...), custom_call_target="tpu_custom_call" | custom-call | tf_op jit(solution)/shard_map/cond/branch_2_fun/exchange312_288/pallas_call | solution.py:629
  108.7 19.0 %unpack.1 = f32[3,8,512,128]{3,2,1,0:T(8,128)} custom-call(s32[4096]{0:T(1024)S(1)} %get-tuple-element.201.meta, f32[8,128]{1,0:T(8,128)S(1)} %get-tuple-element.202.squares, f32[8,1560,128]{2,1,0:T(8,128)} %get-tuple-element.203.recv), custom_call_target="tpu_custom_call" | custom-call | tf_op jit(solution)/shard_map/unpack/pallas_call | solution.py:660
  (1 shorter events, 0.0 us)
Async XLA Ops:
  0.0 20.4 %copy-start.2 = (bf16[256,256]{1,0:T(8,128)(2,1)S(1)}, bf16[256,256]{1,0:T(8,128)(2,1)}, u32[]{:S(2)}) copy-start(bf16[256,256]{1,0:T(8,128)(2,1)} %constant.10.clone.table) | copy-start | bytes 393220
  0.0 20.4 %copy-start = (f32[3,32,64,128]{3,2,1,0:T(8,128)S(1)}, f32[3,32,64,128]{3,2,1,0:T(8,128)}, u32[]{:S(2)}) copy-start(f32[3,32,64,128]{3,2,1,0:T(8,128)} %vel.5) | copy-start | bytes 9437188
  20.4 1.0 copy-start.1
  21.4 0.7 copy-start.3
  22.2 0.7 copy-start.4

commit v4 on v3

--- a/solution.py
+++ b/solution.py
@@ -331,199 +331,209 @@
     lax.fori_loop(0, n_x * half, segment, jnp.int32(0))
 
 
+def halves(n_y):
+    return n_y if n_y % 2 else n_y // 2
+
+
+def plane_order(n_x, n_y, sign):
+    a, b, c = (lax.axis_index(axis) for axis in ("gx", "gy", "wa"))
+    half = halves(n_y)
+    mine = lax.rem(b, half)
+    base = b - mine
+    steps = [(i, j) for i in range(n_x) for j in range(half)]
+
+    def at(base, i, j):
+        x = lax.rem(a + sign * i + n_x, n_x)
+        return (x, base + lax.rem(mine + sign * j + half, half), c)
+
+    near = [at(base, i, j) for i, j in steps]
+    other = lax.rem(base + half, n_y)
+    far = [at(other, i, j) for i, j in steps] if half < n_y else []
+    return near, far
+
+
+def unpack(marks, source, target, lane, at):
+    comps, width = lane.shape
+    group = math.gcd(marks[0].shape[-1], 32)
+    lists, k = marks
+    per_line = lists.shape[2] // group
+
+    def some(t, _):
+        line = lax.div(t, per_line)
+        start = lax.rem(t, per_line) * group
+        for i in range(group):
+            mark = lists[k, line, start + i]
+            fields = jnp.full((comps, width), mark, jnp.int32)
+            ahead = lane + (lax.shift_right_logical(fields, 8) & 255)
+            row = lax.shift_right_logical(mark, 16)
+            head = source[pl.ds(row, comps), :]
+            tail = source[pl.ds(row + comps, comps), :]
+            joined = jnp.where(ahead >= width, head, tail)
+            moved = pltpu.roll(joined, lax.shift_right_logical(mark, 8) & (width - 1), 1)
+            value = jnp.where(lane < (fields & 255), moved, 0.0)
+            target[at, pl.ds((t * group + i) * comps, comps), :] = value
+        return 0
+
+    lax.fori_loop(0, lists.shape[1] * per_line, some, 0)
+
+
 def exchange_kernel(
     n_x, n_y, n_z, comps, rows, direct, extra, send, squares, meta, spill, starts, recv, total, heard,
-    near, far, send_sem, recv_sem, part_send, part_recv, word_send, word_recv, own_sem, *relay,
+    done, near_part, far_part, stage, marks, send_sem, recv_sem, part_send, part_recv, word_send,
+    word_recv, own_sem, done_sem, mark_sem, *rest,
 ):
-    a, b = lax.axis_index("gx"), lax.axis_index("gy")
     c = lax.axis_index("wa")
-    me = a * n_y + b
-    half = max(1, n_y // 2)
-    peers, mates = plane_peers(n_x, n_y), line_mates(n_z)
+    near, far = plane_order(n_x, n_y, 1)
+    me = near[0][0] * n_y + near[0][1]
+    held, relay = rest[: len(near)], rest[len(near) :]
+    peers, mates = near[1:] + far, line_mates(n_z)
     barrier = pltpu.get_barrier_semaphore()
     for device in mates + peers:
         pl.semaphore_signal(barrier, inc=1, device_id=device, device_id_type=MESH)
     pl.semaphore_wait(barrier, len(peers) + len(mates))
 
+    def number(device):
+        return device[0] * n_y + device[1]
+
+    whole = pl.ds(0, rows * comps)
     own = [
-        pltpu.make_async_copy(squares, near.at[c], own_sem.at[0]),
-        pltpu.make_async_copy(meta.at[me], heard.at[me], own_sem.at[1]),
-        pltpu.make_async_copy(
-            send.at[me, pl.ds(0, rows * comps)], recv.at[me, pl.ds(0, rows * comps)], own_sem.at[2]
-        ),
+        pltpu.make_async_copy(squares, near_part.at[c], own_sem.at[0]),
+        pltpu.make_async_copy(meta.at[me], marks.at[0], mark_sem.at[0]),
+        pltpu.make_async_copy(send.at[me, whole], held[0].at[whole], own_sem.at[1]),
     ]
     for copy in own:
         copy.start()
-    copies, relays = [], []
+    first = [
+        send_to(squares, near_part.at[c], part_send.at[k], part_recv.at[k], device)
+        for k, device in enumerate(mates)
+    ]
+    relays, copies, words, blocks = [], [], [], []
     if extra:
         (
-            landed, ready, begins, marks, relay_send, relay_recv, spill_send, spill_recv, begin_sem
+            landed, ready, begins, places, relay_send, relay_recv, spill_send, spill_recv, begin_sem
         ) = relay
-        partner = (a, lax.rem(b + half, n_y), c)
+        tiles = pl.ds(0, extra * comps // 8)
         relays = [
-            send_to(starts, begins, spill_send.at[0], spill_recv.at[0], partner),
-            send_to(
-                spill.at[pl.ds(0, extra * comps // 8)],
-                landed.at[pl.ds(0, extra * comps // 8)],
-                spill_send.at[1],
-                spill_recv.at[1],
-                partner,
-            ),
+            send_to(starts, begins, spill_send.at[0], spill_recv.at[0], far[0]),
+            send_to(spill.at[tiles], landed.at[tiles], spill_send.at[1], spill_recv.at[1], far[0]),
         ]
-    first = [
-        send_to(squares, near.at[c], part_send.at[k], part_recv.at[k], device)
-        for k, device in enumerate(mates)
-    ]
-
-    def number(device):
-        return device[0] * n_y + device[1]
-
-    offsets = plane_offsets(n_x, n_y)
-
-    def blocks_to(k):
-        device = peers[k]
-
-        def go(size):
-            used = pl.ds(0, size * comps)
-            return pltpu.make_async_remote_copy(
-                src_ref=send.at[number(device), used],
-                dst_ref=recv.at[me, used],
-                send_sem=send_sem.at[k],
-                recv_sem=recv_sem.at[k],
-                device_id=device,
-                device_id_type=MESH,
-            )
-
-        if not extra:
-            copy = go(rows)
-            copy.start()
-            return [copy.wait]
-        crosses = lax.div(device[1], half) != lax.div(b, half)
-        inward = lax.div(lax.rem(b - offsets[k][1] + n_y, n_y), half) != lax.div(b, half)
-
-        @pl.when(crosses)
-        def _():
-            go(direct).start()
-
-        @pl.when(jnp.logical_not(crosses))
-        def _():
-            go(rows).start()
-
-        def wait():
-            @pl.when(crosses)
-            def _():
-                go(direct).wait_send()
-
-            @pl.when(jnp.logical_not(crosses))
-            def _():
-                go(rows).wait_send()
-
-            @pl.when(inward)
-            def _():
-                go(direct).wait_recv()
-
-            @pl.when(jnp.logical_not(inward))
-            def _():
-                go(rows).wait_recv()
-
-        return [wait]
-
-    waits = []
     for k, device in enumerate(peers):
-        copies.append(
-            send_to(meta.at[number(device)], heard.at[me], word_send.at[k], word_recv.at[k], device)
+        words.append(
+            send_to(meta.at[number(device)], heard.at[k + 1], word_send.at[k], word_recv.at[k], device)
         )
-    ahead = min(3, len(peers))
-    for k in range(ahead):
-        waits += blocks_to(k)
+    short = pl.ds(0, direct * comps) if extra else whole
+    for k, device in enumerate(peers):
+        if k + 1 < len(near):
+            used, target = whole, held[k + 1].at[whole]
+        else:
+            used, target = short, recv.at[k + 1 - len(near), short]
+        blocks.append(
+            send_to(send.at[number(device), used], target, send_sem.at[k], recv_sem.at[k], device)
+        )
     own[0].wait()
     for copy in first:
         copy.wait()
     for k, device in enumerate(peers):
         sem = n_z - 1 + k
-        copies.append(send_to(near, far.at[k], part_send.at[sem], part_recv.at[sem], device))
-    for k in range(ahead, len(peers)):
-        waits += blocks_to(k)
+        copies.append(
+            send_to(near_part, far_part.at[k], part_send.at[sem], part_recv.at[sem], device)
+        )
     if extra:
         relays[0].wait()
-        load = pltpu.make_async_copy(begins, marks, begin_sem.at[0])
+        load = pltpu.make_async_copy(begins, places, begin_sem.at[0])
         load.start()
         load.wait()
         relays[1].wait()
         size = (rows - direct) * comps
-        source = a * n_y + lax.rem(b + half, n_y)
-        mine = lax.rem(b, half)
-        base = b - mine
-        places = [
-            (lax.rem(a + i, n_x), lax.rem(mine + j, half)) for i in range(n_x) for j in range(half)
-        ]
-        for k, (x, y) in enumerate(places):
-            begin = marks[0, x * half + y] * comps
+        half = halves(n_y)
+        for k, (x, y, _) in enumerate(near):
+            begin = places[0, x * half + lax.rem(y, half)] * comps
 
             def tile(i, _, k=k, begin=begin):
                 ready[k, pl.ds(pl.multiple_of(i * 8, 8), 8), :] = landed[begin + i]
                 return 0
 
             lax.fori_loop(0, size // 8, tile, 0)
-        spot = recv.at[source, pl.ds(direct * comps, size)]
-        for k, (x, y) in enumerate(places):
+        past = pl.ds(direct * comps, size)
+        for k, device in enumerate(near):
             if k:
                 copies.append(
-                    send_to(ready.at[k], spot, relay_send.at[k], relay_recv.at[k], (x, base + y, c))
+                    send_to(
+                        ready.at[k], recv.at[k, past], relay_send.at[k], relay_recv.at[k], device
+                    )
                 )
-        keep = pltpu.make_async_copy(ready.at[0], spot, begin_sem.at[1])
+        keep = pltpu.make_async_copy(ready.at[0], recv.at[0, past], begin_sem.at[1])
         keep.start()
         keep.wait()
-    for copy in own[1:]:
+    lane = lax.broadcasted_iota(jnp.int32, (comps, send.shape[2]), 1)
+    outs = []
+    for k in range(len(near)):
+        if k:
+            words[k - 1].wait()
+            load = pltpu.make_async_copy(heard.at[k], marks.at[k], mark_sem.at[k])
+            load.start()
+            load.wait()
+            blocks[k - 1].wait()
+        else:
+            own[1].wait()
+            own[2].wait()
+        unpack((marks, k), held[k], stage, lane, k)
+        out = pltpu.make_async_copy(stage.at[k], done.at[k], done_sem.at[k])
+        out.start()
+        outs.append(out)
+    for copy in words[len(near) - 1 :] + blocks[len(near) - 1 :] + copies + outs:
         copy.wait()
-    for copy in copies:
-        copy.wait()
-    for wait in waits:
-        wait()
-    total[...] = jnp.sum(near[...], axis=0) + jnp.sum(far[...], axis=(0, 1))
-
-
-def unpack_kernel(every, meta, squares, recv, out, scale):
+    total[...] = jnp.sum(near_part[...], axis=0) + jnp.sum(far_part[...], axis=(0, 1))
+
+
+def finish_kernel(every, near, order, meta, squares, recv, done, out, scale):
     comps, _, capacity, width = out.shape
-    source = pl.program_id(0)
-
-    @pl.when(source == 0)
+    step = pl.program_id(0)
+
+    @pl.when(step == 0)
     def _():
         total = jnp.sum(squares[...], keepdims=True)
         scale[...] = jnp.broadcast_to(1.0 / jnp.sqrt(total / every + 1e-06), scale.shape)
 
-    lane = lax.broadcasted_iota(jnp.int32, (comps, width), 1)
-    factor = scale[:comps]
-    group = math.gcd(capacity, 32)
-    first = source * capacity
-
-    def some(t, _):
-        start = first + t * group
-        for k in range(group):
-            mark = meta[start + k]
-            fields = jnp.full((comps, width), mark, jnp.int32)
-            ahead = lane + (lax.shift_right_logical(fields, 8) & 255)
-            row = lax.shift_right_logical(mark, 16)
-            head = recv[0, pl.ds(row, comps), :]
-            tail = recv[0, pl.ds(row + comps, comps), :]
-            joined = jnp.where(ahead >= width, head, tail)
-            moved = pltpu.roll(joined, lax.shift_right_logical(mark, 8) & (width - 1), 1)
-            value = jnp.where(lane < (fields & 255), moved * factor, 0.0)
-            for c in range(comps):
-                out[c, 0, pl.ds(t * group + k, 1), :] = value[c : c + 1]
-        return 0
-
-    lax.fori_loop(0, capacity // group, some, 0)
+    @pl.when(step < near)
+    def _():
+        for c in range(comps):
+            out[c, 0] = done[0, pl.ds(c, capacity, stride=comps), :] * scale[:1]
+
+    @pl.when(step >= near)
+    def _():
+        lane = lax.broadcasted_iota(jnp.int32, (comps, width), 1)
+        factor = scale[:comps]
+        group = math.gcd(capacity, 64)
+        first = step * capacity
+
+        def some(t, _):
+            start = first + t * group
+            for k in range(group):
+                mark = meta[start + k]
+                fields = jnp.full((comps, width), mark, jnp.int32)
+                ahead = lane + (lax.shift_right_logical(fields, 8) & 255)
+                row = lax.shift_right_logical(mark, 16)
+                head = recv[0, pl.ds(row, comps), :]
+                tail = recv[0, pl.ds(row + comps, comps), :]
+                joined = jnp.where(ahead >= width, head, tail)
+                moved = pltpu.roll(joined, lax.shift_right_logical(mark, 8) & (width - 1), 1)
+                value = jnp.where(lane < (fields & 255), moved * factor, 0.0)
+                for c in range(comps):
+                    out[c, 0, pl.ds(t * group + k, 1), :] = value[c : c + 1]
+            return 0
+
+        lax.fori_loop(0, capacity // group, some, 0)
 
 
 def tier_sizes(capacity, n_y):
     def up(part):
         return -(-capacity * part // (64 * 8)) * 8
 
-    direct = [(up(part), 0) for part in (48, 56, 64)]
+    direct = [(up(part), 0) for part in (52, 64)]
     if n_y % 2:
         return up(64), direct
-    parts = ((38, 28), (38, 32), (39, 36), (40, 44), (44, 52))
+    parts = ((38, 28), (39, 36), (40, 44), (44, 54))
     spilled = [(up(rows), up(extra)) for rows, extra in parts]
     return up(18), spilled + direct
 
@@ -539,7 +549,8 @@
     f32 = jnp.float32
     direct, tiers = tier_sizes(capacity, n_y)
     most_extra = max([8] + [extra for _, extra in tiers])
-    senders = n_x * max(1, n_y // 2)
+    senders = n_x * halves(n_y)
+    beyond = max(1, writers - senders)
 
     smem = pl.BlockSpec(memory_space=pltpu.SMEM)
     vmem = pl.BlockSpec(memory_space=pltpu.VMEM)
@@ -615,6 +626,7 @@
     def exchange(index, *operands):
         rows, extra = tiers[index]
         size = (rows - direct) * comps
+        held = [pltpu.VMEM(((rows + 8) * comps, width), f32) for _ in range(senders)]
         relay = [
             pltpu.VMEM(((extra * comps + size) // 8, 8, width), f32),
             pltpu.VMEM((senders, size, width), f32),
@@ -629,47 +641,69 @@
         return pl.pallas_call(
             functools.partial(exchange_kernel, n_x, n_y, n_z, comps, rows, direct, extra),
             out_shape=(
-                jax.ShapeDtypeStruct(outgoing.shape, f32),
+                jax.ShapeDtypeStruct((beyond, region * comps, width), f32),
                 jax.ShapeDtypeStruct(squares.shape, f32),
                 jax.ShapeDtypeStruct(meta.shape, jnp.int32),
+                jax.ShapeDtypeStruct((senders, capacity * comps, width), f32),
             ),
             in_specs=[anywhere, vmem, anywhere, anywhere, anywhere],
-            out_specs=(anywhere, vmem, anywhere),
+            out_specs=(anywhere, vmem, anywhere, anywhere),
             scratch_shapes=[
                 pltpu.VMEM((n_z,) + squares.shape, f32),
                 pltpu.VMEM((writers - 1, n_z) + squares.shape, f32),
+                pltpu.VMEM((senders, capacity * comps, width), f32),
+                pltpu.SMEM((senders,) + meta.shape[1:], jnp.int32),
                 dma((writers - 1,)),
                 dma((writers - 1,)),
                 dma((writers + n_z - 2,)),
                 dma((writers + n_z - 2,)),
                 dma((writers - 1,)),
                 dma((writers - 1,)),
-                dma((3,)),
+                dma((2,)),
+                dma((senders,)),
+                dma((senders,)),
             ]
+            + held
             + (relay if extra else []),
-            compiler_params=pltpu.CompilerParams(collective_id=2 + index, has_side_effects=True),
+            compiler_params=pltpu.CompilerParams(
+                collective_id=2 + index, has_side_effects=True, vmem_limit_bytes=48 * 2**20
+            ),
             name=f"exchange{rows}_{extra}",
         )(*operands)
 
     branches = [functools.partial(exchange, index) for index in range(len(tiers))]
-    arrived, squares, heard = lax.switch(
+    arrived, squares, heard, done = lax.switch(
         tier[0], branches, outgoing, squares, meta, spill, starts.reshape(1, 128)
     )
 
+    near, far = plane_order(n_x, n_y, -1)
+    order = jnp.stack([x * n_y + y for x, y, _ in near + far]).astype(jnp.int32)
     every = velocity.size * n_x * n_y * n_z
     received = pl.pallas_call(
-        functools.partial(unpack_kernel, float(every)),
-        grid=(writers,),
-        in_specs=[
-            smem,
-            pl.BlockSpec((8, cells_z), lambda s: (0, 0)),
-            pl.BlockSpec((1, region * comps, width), lambda s: (s, 0, 0)),
-        ],
-        out_specs=pl.BlockSpec((comps, 1, capacity, width), lambda s: (0, s, 0, 0)),
+        functools.partial(finish_kernel, float(every), senders),
+        grid_spec=pltpu.PrefetchScalarGridSpec(
+            num_scalar_prefetch=1,
+            grid=(writers,),
+            in_specs=[
+                smem,
+                pl.BlockSpec((8, cells_z), lambda s, order: (0, 0)),
+                pl.BlockSpec(
+                    (1, region * comps, width),
+                    lambda s, order: (jnp.maximum(s - senders, 0), 0, 0),
+                ),
+                pl.BlockSpec(
+                    (1, capacity * comps, width),
+                    lambda s, order: (jnp.minimum(s, senders - 1), 0, 0),
+                ),
+            ],
+            out_specs=pl.BlockSpec(
+                (comps, 1, capacity, width), lambda s, order: (0, order[s], 0, 0)
+            ),
+            scratch_shapes=[pltpu.VMEM((8, width), f32)],
+        ),
         out_shape=jax.ShapeDtypeStruct((comps, writers, capacity, width), f32),
-        scratch_shapes=[pltpu.VMEM((8, width), f32)],
-        name="unpack",
-    )(heard.reshape(writers * capacity), squares, arrived)
+        name="finish",
+    )(order, heard.reshape(writers * capacity), squares, arrived, done)
     return received.reshape(1, 1, comps, writers, capacity, width)
 
 

time: 130 us -> 119 us (0.915); the launches traced: 128 us -> 119 us
  Pallas kernels: 125 us -> 116 us
    pallas_call x1, Pallas kernels: 19 us -> 11.8 us  [local(): pl.pallas_call(functools.partial(finish_kernel, float(every), senders), g...]
    pallas_call x1, Pallas kernels: 18.6 us -> 16.8 us  [local(): pl.pallas_call(functools.partial(blocks_kernel, n_x, n_y, region, direct)...]
    unnamed x10, local copies, waits for them, and re-layouts: 2.41 us -> 1 us
where the time goes in v4:
time: 119 us
  Pallas kernels  116 us (97%)
  local copies, waits for them, and re-layouts  1.61 us (1%)
    pallas_call x1, Pallas kernels, exchange(): pl.pallas_call(functools.partial(exchange_kernel, n_x, n_y, n_z, comps, r...  67.9 us
    pallas_call x1, Pallas kernels, local(): pl.pallas_call(functools.partial(blocks_kernel, n_x, n_y, region, direct)...  16.8 us
    pallas_call x1, Pallas kernels, local(): pl.pallas_call(functools.partial(halo_kernel, (n_x, n_y, n_z), tiers), ou...  15.1 us
    pallas_call x1, Pallas kernels, local(): pl.pallas_call(functools.partial(finish_kernel, float(every), senders), g...  11.8 us
    pallas_call x1, Pallas kernels, local(): pl.pallas_call(functools.partial(faces_kernel, writers, capacity, region,...  4.63 us

profile of v4, /device:TPU:0, one launch (start us, length us, event | category | flops | bytes accessed | tf_op | source)
XLA Modules:
  0.0 118.6 jit_solution(3091535879706786934)
XLA Ops:
  0.0 0.0 copy-start
  0.0 0.0 copy-start.2
  0.0 4.6 %faces.1 = (s32[3,16,128]{2,1,0:T(8,128)}, s32[8,128]{1,0:T(8,128)}, f32[2,2,32,128]{3,2,1,0:T(8,128)}, f32[2,2,64,128]{3,2,1,0:T(8,128)}, f32[8,128]{1,0:T(8,128)}) custom-call(s32[16,128]{1,0:T(8,128)} %bitcast.37, s32[16,128]{1,0:T(8,128)} %bitcast.38, f32[3,32,64,128]{3,2,1,0:T(8,128)} %vel.5), custom_call_target="tpu_custom_call" | custom-call | tf_op jit(solution)/shard_map/faces/pallas_call | solution.py:559
  4.6 0.0 copy-start.3
  4.6 0.0 copy-start.4
  4.6 15.1 %halo.1 = (f32[6,2,64,128]{3,2,1,0:T(8,128)}, s32[1]{0:T(128)}) custom-call(f32[3,32,64,128]{3,2,1,0:T(8,128)} %vel.5, f32[2,2,32,128]{3,2,1,0:T(8,128)} %get-tuple-element.141.y_faces, f32[2,2,64,128]{3,2,1,0:T(8,128)} %get-tuple-element.142.z_faces, f32[8,128]{1,0:T(8,128)} %get-tuple-element.143.need), custom_call_target="tpu_custom_call" | custom-call | tf_op jit(solution)/shard_map/halo/pallas_call | solution.py:571
  19.8 0.0 copy-done
  19.8 0.0 copy-done.2
  19.8 0.0 copy-done.3
  19.8 0.0 copy-done.4
  19.8 0.0 copy-start.1
  19.8 1.0 copy-done.1
  20.8 16.8 %blocks.1 = (f32[12480,128]{1,0:T(8,128)S(1)}, f32[8,128]{1,0:T(8,128)S(1)}, s32[4096]{0:T(1024)S(1)}, f32[162,8,128]{2,1,0:T(8,128)S(1)}, s32[128]{0:T(128)S(1)}) custom-call(s32[6144]{0:T(1024)S(1)} %bitcast.17, s32[8,128]{1,0:T(8,128)S(1)} %copy-done.4, s32[4096]{0:T(1024)S(1)} %broadcast_in_dim.3.blank, f32[3,32,64,128]{3,2,1,0:T(8,128)S(1)} %copy-done, ...), custom_call_target="tpu_custom_call" | custom-call | tf_op jit(solution)/shard_map/blocks/pallas_call | solution.py:593
  38.2 67.9 %conditional.1 = ((f32[4,1560,128]{2,1,0:T(8,128)S(1)}, f32[8,128]{1,0:T(8,128)S(1)}, s32[8,4,128]{2,1,0:T(4,128)S(1)}, f32[4,1536,128]{2,1,0:T(8,128)})) conditional(s32[]{:T(128)} %bitcast.10, (f32[8,1560,128]{2,1,0:T(8,128)S(1)}, f32[8,128]{1,0:T(8,128)S(1)}, s32[8,4,128]{2,1,0:T(4,128)S(1)}, ...), branch_computations={%region_0.0_spmd, %region_1.0_spmd, %region_2.0_spmd, %region_3.0_... | conditional | bytes 8 | solution.py:675
  38.2 67.9 %exchange312_288.1 = (f32[4,1560,128]{2,1,0:T(8,128)S(1)}, f32[8,128]{1,0:T(8,128)S(1)}, s32[8,4,128]{2,1,0:T(4,128)S(1)}, f32[4,1536,128]{2,1,0:T(8,128)}) custom-call(f32[8,1560,128]{2,1,0:T(8,128)S(1)} %get-tuple-element.100.send, f32[8,128]{1,0:T(8,128)S(1)} %get-tuple-element.101.squares, s32[8,4,128]{2,1,0:T(4,128)S(1)} %get-tuple-element.102.meta, ...), custom_call_target="tpu_custom_call" | custom-call | tf_op jit(solution)/shard_map/cond/branch_1_fun/exchange312_288/pallas_call | solution.py:641
  106.2 0.6 stack.35.order
  106.8 11.8 %finish.1 = f32[3,8,512,128]{3,2,1,0:T(8,128)} custom-call(s32[8]{0:T(128)} %stack.35.order, s32[4096]{0:T(1024)S(1)} %bitcast.36, f32[8,128]{1,0:T(8,128)S(1)} %get-tuple-element.185.squares, f32[4,1560,128]{2,1,0:T(8,128)S(1)} %get-tuple-element.186.recv, f32[4,1536,128]{2,1,0:T(8,128)} %get-tuple-element.184.done), custom_call_target="tpu_custom_call" | custom-call | tf_op jit(solution)/shard_map/finish/pallas_call | solution.py:682
  (1 shorter events, 0.0 us)
Async XLA Ops:
  0.0 19.8 %copy-start = (f32[3,32,64,128]{3,2,1,0:T(8,128)S(1)}, f32[3,32,64,128]{3,2,1,0:T(8,128)}, u32[]{:S(2)}) copy-start(f32[3,32,64,128]{3,2,1,0:T(8,128)} %vel.5) | copy-start | bytes 9437188
  0.0 19.8 %copy-start.2 = (bf16[256,256]{1,0:T(8,128)(2,1)S(1)}, bf16[256,256]{1,0:T(8,128)(2,1)}, u32[]{:S(2)}) copy-start(bf16[256,256]{1,0:T(8,128)(2,1)} %constant.42.clone.table) | copy-start | bytes 393220
  4.6 15.2 %copy-start.3 = (s32[3,16,128]{2,1,0:T(8,128)S(1)}, s32[3,16,128]{2,1,0:T(8,128)}, u32[]{:S(2)}) copy-start(s32[3,16,128]{2,1,0:T(8,128)} %get-tuple-element.145) | copy-start | bytes 73732
  4.6 15.2 %copy-start.4 = (s32[8,128]{1,0:T(8,128)S(1)}, s32[8,128]{1,0:T(8,128)}, u32[]{:S(2)}) copy-start(s32[8,128]{1,0:T(8,128)} %get-tuple-element.146.tallies) | copy-start | bytes 12292
  19.8 1.0 copy-start.1

commit v5 on v4

--- a/solution.py
+++ b/solution.py
@@ -32,32 +32,7 @@
     return lax.shift_right_logical(jnp.maximum(used - direct, 0) + 7, 3)
 
 
-def faces_kernel(
-    writers, capacity, region, direct, n_y, targets, lens, vel, plan, counts, y_faces, z_faces, need,
-    sums
-):
-    comps, cells_x, cells_y, cells_z = vel.shape
-    lane = lax.broadcasted_iota(jnp.int32, (cells_y, cells_z), 1)
-
-    def plane(x, acc):
-        here = lane == x
-        rolled = [
-            pltpu.roll(vel[comp, x], lax.rem(x + last, cells_z), 1)
-            for last in range(2)
-            for comp in (0, 1)
-        ]
-        for i, comp in enumerate((0, 2)):
-            y_faces[0, i, pl.ds(x, 1), :] = vel[comp, x, 0:1]
-            y_faces[1, i, pl.ds(x, 1), :] = vel[comp, x, cells_y - 1 : cells_y]
-        return tuple(jnp.where(here, new, old) for new, old in zip(rolled, acc))
-
-    zero = jnp.zeros((cells_y, cells_z), jnp.float32)
-    columns = lax.fori_loop(0, cells_x, plane, (zero,) * 4, unroll=4)
-    for last in range(2):
-        for i in range(2):
-            z_faces[last, i] = columns[2 * last + i]
-
-    t, kept = targets[...], lens[...]
+def plan_blocks(writers, capacity, region, direct, n_y, comps, t, kept, plan, counts, need, sums):
     rows, lanes = t.shape
     shape = (lanes, lanes)
     upper = (
@@ -89,11 +64,6 @@
 
     none = jnp.zeros_like(t)
     spot, start, site = lax.fori_loop(0, writers, body, (none, none, none), unroll=8)
-    shift = start & (lanes - 1)
-    row = lax.shift_right_logical(start, lanes.bit_length() - 1)
-    plan[2] = spot
-    plan[0] = (row + site) * (comps << 16) + shift
-    plan[1] = row * (comps << 16) + (lanes - shift) * 256 + kept
     used = jnp.sum(sums[...], axis=1, keepdims=True).astype(jnp.int32)
     used = jnp.broadcast_to(lax.shift_right_logical(used + (lanes - 1), 7), counts.shape)
     counts[...] = used
@@ -105,6 +75,11 @@
     extra = jnp.sum(over.astype(jnp.float32), axis=0, keepdims=True)
     line = lax.broadcasted_iota(jnp.int32, need.shape, 0)
     need[...] = jnp.where(line == 0, most, jnp.where(line == 1, extra, 0.0))
+    shift = start & (lanes - 1)
+    row = lax.shift_right_logical(start, lanes.bit_length() - 1)
+    plan[2] = spot
+    plan[0] = (row + site) * (comps << 16) + shift
+    plan[1] = row * (comps << 16) + (lanes - shift) * 256 + kept
 
 
 def plane_offsets(n_x, n_y):
@@ -135,54 +110,94 @@
     return copy
 
 
-def halo_kernel(
-    sizes, tiers, vel, y_faces, z_faces, need, halos, tier, near, far, send_sem, recv_sem, part_send,
-    part_recv, own_sem,
+def spill_tiles(used, direct):
+    return lax.shift_right_logical(jnp.maximum(used - direct, 0) + 7, 3)
+
+
+def front_kernel(
+    sizes, tiers, capacity, region, direct, targets, lens, vel, plan, counts, halos, tier, order,
+    z_faces, need, sums, near_part, far_part, send_sem, recv_sem, part_send, part_recv, own_sem,
 ):
     place = [lax.axis_index(axis) for axis in ("gx", "gy", "wa")]
     n_x, n_y, n_z = sizes
-    cells_x = vel.shape[1]
+    comps, cells_x, cells_y, cells_z = vel.shape
+    writers = n_x * n_y
 
     def beside(axis, step):
         size = sizes[axis]
         moved = lax.rem(place[axis] + step + size, size)
         return tuple(moved if i == axis else p for i, p in enumerate(place))
 
-    across, along = pl.ds(0, vel.shape[2]), pl.ds(0, cells_x)
+    across, along = pl.ds(0, cells_y), pl.ds(0, cells_x)
+    peers, mates = plane_peers(n_x, n_y), line_mates(n_z)
+    others = [beside(axis, step) for axis in range(3) for step in (1, -1)] + peers + mates
+    barrier = pltpu.get_barrier_semaphore()
+    for device in others:
+        pl.semaphore_signal(barrier, inc=1, device_id=device, device_id_type=MESH)
+    plan_blocks(
+        writers, capacity, region, direct, n_y, comps, targets[...], lens[...], plan, counts, need,
+        sums,
+    )
+    pl.semaphore_wait(barrier, len(others))
     moves = [
         (vel.at[pl.ds(1, 2), cells_x - 1], halos.at[0, :, across], beside(0, 1)),
         (vel.at[pl.ds(1, 2), 0], halos.at[1, :, across], beside(0, -1)),
-        (y_faces.at[1], halos.at[2, :, along], beside(1, 1)),
-        (y_faces.at[0], halos.at[3, :, along], beside(1, -1)),
-        (z_faces.at[1], halos.at[4, :, across], beside(2, 1)),
-        (z_faces.at[0], halos.at[5, :, across], beside(2, -1)),
     ]
-    peers, mates = plane_peers(n_x, n_y), line_mates(n_z)
-    others = [device for _, _, device in moves] + peers + mates
-    barrier = pltpu.get_barrier_semaphore()
-    for device in others:
-        pl.semaphore_signal(barrier, inc=1, device_id=device, device_id_type=MESH)
-    pl.semaphore_wait(barrier, len(others))
-    c = place[2]
-    own = pltpu.make_async_copy(need, near.at[c], own_sem)
-    own.start()
-    first = [
-        send_to(need, near.at[c], part_send.at[k], part_recv.at[k], device)
-        for k, device in enumerate(mates)
-    ]
+    for i, comp in enumerate((0, 2)):
+        moves += [
+            (vel.at[comp, :, cells_y - 1], halos.at[2, i, along], beside(1, 1)),
+            (vel.at[comp, :, 0], halos.at[3, i, along], beside(1, -1)),
+        ]
     copies = [
         send_to(src, dst, send_sem.at[k], recv_sem.at[k], device)
         for k, (src, dst, device) in enumerate(moves)
     ]
+    c = place[2]
+    own = pltpu.make_async_copy(need, near_part.at[c], own_sem)
+    own.start()
+    first = [
+        send_to(need, near_part.at[c], part_send.at[k], part_recv.at[k], device)
+        for k, device in enumerate(mates)
+    ]
+    lane = lax.broadcasted_iota(jnp.int32, (cells_y, cells_z), 1)
+
+    def plane(x, acc):
+        here = lane == x
+        rolled = [
+            pltpu.roll(vel[comp, x], lax.rem(x + last, cells_z), 1)
+            for last in range(2)
+            for comp in (0, 1)
+        ]
+        return tuple(jnp.where(here, new, old) for new, old in zip(rolled, acc))
+
+    zero = jnp.zeros((cells_y, cells_z), jnp.float32)
+    columns = lax.fori_loop(0, cells_x, plane, (zero,) * 4, unroll=4)
+    for last in range(2):
+        for i in range(2):
+            z_faces[last, i] = columns[2 * last + i]
+    near, far = plane_order(n_x, n_y, -1)
+    for k, (x, y, _) in enumerate(near + far):
+        order[k] = x * n_y + y
     own.wait()
     for copy in first:
         copy.wait()
     for k, device in enumerate(peers):
         sem = n_z - 1 + k
-        copies.append(send_to(near, far.at[k], part_send.at[sem], part_recv.at[sem], device))
+        copies.append(
+            send_to(near_part, far_part.at[k], part_send.at[sem], part_recv.at[sem], device)
+        )
+    k = len(moves)
+    for src, spot, step in ((1, 4, 1), (0, 5, -1)):
+        copies.append(
+            send_to(
+                z_faces.at[src], halos.at[spot, :, across], send_sem.at[k], recv_sem.at[k],
+                beside(2, step),
+            )
+        )
+        k += 1
     for copy in copies:
         copy.wait()
-    most = jnp.maximum(jnp.max(near[...], axis=0), jnp.max(far[...], axis=(0, 1)))
+    most = jnp.maximum(jnp.max(near_part[...], axis=0), jnp.max(far_part[...], axis=(0, 1)))
     pair, extra = jnp.max(most[0:1]), jnp.max(most[1:2])
     chosen = jnp.int32(len(tiers) - 1)
     for index in reversed(range(len(tiers) - 1)):
@@ -352,9 +367,9 @@
     return near, far
 
 
-def unpack(marks, source, target, lane, at):
+def unpack(count, marks, source, target, lane, at):
     comps, width = lane.shape
-    group = math.gcd(marks[0].shape[-1], 32)
+    group = math.gcd(marks[0].shape[-1], 32 if count <= 4 else 8)
     lists, k = marks
     per_line = lists.shape[2] // group
 
@@ -477,7 +492,7 @@
         else:
             own[1].wait()
             own[2].wait()
-        unpack((marks, k), held[k], stage, lane, k)
+        unpack(len(near), (marks, k), held[k], stage, lane, k)
         out = pltpu.make_async_copy(stage.at[k], done.at[k], done_sem.at[k])
         out.start()
         outs.append(out)
@@ -533,7 +548,7 @@
     direct = [(up(part), 0) for part in (52, 64)]
     if n_y % 2:
         return up(64), direct
-    parts = ((38, 28), (39, 36), (40, 44), (44, 54))
+    parts = ((38, 28), (39, 36), (39, 44), (40, 54))
     spilled = [(up(rows), up(extra)) for rows, extra in parts]
     return up(18), spilled + direct
 
@@ -556,38 +571,34 @@
     vmem = pl.BlockSpec(memory_space=pltpu.VMEM)
     anywhere = pl.BlockSpec(memory_space=pl.ANY)
     dma = pltpu.SemaphoreType.DMA
-    plan, tallies, y_faces, z_faces, need = pl.pallas_call(
-        functools.partial(faces_kernel, writers, capacity, region, direct, n_y),
+    plan, tallies, halos, tier, order = pl.pallas_call(
+        functools.partial(front_kernel, (n_x, n_y, n_z), tiers, capacity, region, direct),
         out_shape=(
             jax.ShapeDtypeStruct((3, nblk // 128, 128), jnp.int32),
             jax.ShapeDtypeStruct((writers, 128), jnp.int32),
-            jax.ShapeDtypeStruct((2, 2, cells_x, cells_z), f32),
-            jax.ShapeDtypeStruct((2, 2, cells_y, cells_z), f32),
-            jax.ShapeDtypeStruct((8, 128), f32),
-        ),
-        scratch_shapes=[pltpu.VMEM((writers, 128), f32)],
-        name="faces",
-    )(destinations.reshape(nblk // 128, 128), lengths.reshape(nblk // 128, 128), velocity)
-    halos, tier = pl.pallas_call(
-        functools.partial(halo_kernel, (n_x, n_y, n_z), tiers),
-        out_shape=(
             jax.ShapeDtypeStruct((6, 2, max(cells_x, cells_y), cells_z), f32),
             jax.ShapeDtypeStruct((1,), jnp.int32),
+            jax.ShapeDtypeStruct((writers,), jnp.int32),
         ),
-        in_specs=[anywhere] * 3 + [vmem],
-        out_specs=(anywhere, smem),
+        in_specs=[vmem, vmem, vmem],
+        out_specs=(vmem, vmem, vmem, smem, smem),
         scratch_shapes=[
-            pltpu.VMEM((n_z,) + need.shape, f32),
-            pltpu.VMEM((writers - 1, n_z) + need.shape, f32),
-            dma((6,)),
-            dma((6,)),
+            pltpu.VMEM((2, 2, cells_y, cells_z), f32),
+            pltpu.VMEM((8, 128), f32),
+            pltpu.VMEM((writers, 128), f32),
+            pltpu.VMEM((n_z, 8, 128), f32),
+            pltpu.VMEM((writers - 1, n_z, 8, 128), f32),
+            dma((8,)),
+            dma((8,)),
             dma((writers + n_z - 2,)),
             dma((writers + n_z - 2,)),
             dma,
         ],
-        compiler_params=pltpu.CompilerParams(collective_id=1, has_side_effects=True),
-        name="halo",
-    )(velocity, y_faces, z_faces, need)
+        compiler_params=pltpu.CompilerParams(
+            collective_id=1, has_side_effects=True, vmem_limit_bytes=16 * 2**20
+        ),
+        name="front",
+    )(destinations.reshape(nblk // 128, 128), lengths.reshape(nblk // 128, 128), velocity)
 
     table = jnp.asarray(split_table())
     outgoing, squares, meta, spill, starts = pl.pallas_call(
@@ -676,8 +687,6 @@
         tier[0], branches, outgoing, squares, meta, spill, starts.reshape(1, 128)
     )
 
-    near, far = plane_order(n_x, n_y, -1)
-    order = jnp.stack([x * n_y + y for x, y, _ in near + far]).astype(jnp.int32)
     every = velocity.size * n_x * n_y * n_z
     received = pl.pallas_call(
         functools.partial(finish_kernel, float(every), senders),

time: 119 us -> 118 us (level); the launches traced: 119 us -> 120 us
  local copies, waits for them, and re-layouts: 1.61 us -> 4.19 us
    pallas_call x2 -> x1, Pallas kernels: 19.7 us -> 14.5 us  [local(): pl.pallas_call(functools.partial(front_kernel, (n_x, n_y, n_z), tiers, ca...]
    pallas_call x1, Pallas kernels: 67.9 us -> 71.5 us  [exchange(): pl.pallas_call(functools.partial(exchange_kernel, n_x, n_y, n_z, comps, r...]
    unnamed x10 -> x12, local copies, waits for them, and re-layouts: 1 us -> 4.19 us
where the time goes in v5:
time: 118 us; the launch traced here: 120 us
  Pallas kernels  115 us (97%)
  local copies, waits for them, and re-layouts  4.19 us (4%)
    pallas_call x1, Pallas kernels, exchange(): pl.pallas_call(functools.partial(exchange_kernel, n_x, n_y, n_z, comps, r...  71.5 us
    pallas_call x1, Pallas kernels, local(): pl.pallas_call(functools.partial(blocks_kernel, n_x, n_y, region, direct)...  16.7 us
    pallas_call x1, Pallas kernels, local(): pl.pallas_call(functools.partial(front_kernel, (n_x, n_y, n_z), tiers, ca...  14.5 us
    pallas_call x1, Pallas kernels, local(): pl.pallas_call(functools.partial(finish_kernel, float(every), senders), g...  12.1 us
    unnamed x12, local copies, waits for them, and re-layouts  4.19 us

profile of v5, /device:TPU:0, one launch (start us, length us, event | category | flops | bytes accessed | tf_op | source)
XLA Modules:
  0.0 119.7 jit_solution(17042958129898539657)
XLA Ops:
  0.0 0.0 copy-start
  0.0 1.9 %copy-done = f32[3,32,64,128]{3,2,1,0:T(8,128)S(1)} copy-done((f32[3,32,64,128]{3,2,1,0:T(8,128)S(1)}, f32[3,32,64,128]{3,2,1,0:T(8,128)}, u32[]{:S(2)}) %copy-start) | copy-done | bytes 3145752
  1.9 0.0 copy-start.3
  1.9 0.7 copy-done.3
  2.6 0.0 copy-start.4
  2.6 0.7 copy-done.4
  3.3 0.0 copy-start.1
  3.3 14.5 %front.1 = (s32[3,16,128]{2,1,0:T(8,128)S(1)}, s32[8,128]{1,0:T(8,128)S(1)}, f32[6,2,64,128]{3,2,1,0:T(8,128)S(1)}, s32[1]{0:T(128)}, s32[8]{0:T(128)S(1)}) custom-call(s32[16,128]{1,0:T(8,128)S(1)} %bitcast.10, s32[16,128]{1,0:T(8,128)S(1)} %bitcast.11, f32[3,32,64,128]{3,2,1,0:T(8,128)S(1)} %copy-done), custom_call_target="tpu_custom_call" | custom-call | tf_op jit(solution)/shard_map/front/pallas_call | solution.py:574
  17.8 0.0 copy-start.5
  18.4 0.0 copy-done.5
  18.5 0.0 copy-done.1
  18.5 0.0 copy-start.2
  18.5 0.9 copy-done.2
  19.4 16.7 %blocks.1 = (f32[12480,128]{1,0:T(8,128)S(1)}, f32[8,128]{1,0:T(8,128)S(1)}, s32[4096]{0:T(1024)S(1)}, f32[162,8,128]{2,1,0:T(8,128)S(1)}, s32[128]{0:T(128)S(1)}) custom-call(s32[6144]{0:T(1024)S(1)} %bitcast.9, s32[8,128]{1,0:T(8,128)S(1)} %get-tuple-element.142.tallies, s32[4096]{0:T(1024)S(1)} %broadcast_in_dim.3.blank, ...), custom_call_target="tpu_custom_call" | custom-call | tf_op jit(solution)/shard_map/blocks/pallas_call | solution.py:604
  36.1 71.5 %conditional.1 = ((f32[4,1560,128]{2,1,0:T(8,128)}, f32[8,128]{1,0:T(8,128)S(1)}, s32[8,4,128]{2,1,0:T(4,128)S(1)}, f32[4,1536,128]{2,1,0:T(8,128)})) conditional(s32[]{:T(128)} %bitcast.2, (f32[8,1560,128]{2,1,0:T(8,128)S(1)}, f32[8,128]{1,0:T(8,128)S(1)}, s32[8,4,128]{2,1,0:T(4,128)S(1)}, ...), branch_computations={%region_0.0_spmd, %region_1.0_spmd, %region_2.0_spmd, %region_3.0_... | conditional | bytes 8 | solution.py:686
  36.2 71.5 %exchange312_352.1 = (f32[4,1560,128]{2,1,0:T(8,128)}, f32[8,128]{1,0:T(8,128)S(1)}, s32[8,4,128]{2,1,0:T(4,128)S(1)}, f32[4,1536,128]{2,1,0:T(8,128)}) custom-call(f32[8,1560,128]{2,1,0:T(8,128)S(1)} %get-tuple-element.105.send, f32[8,128]{1,0:T(8,128)S(1)} %get-tuple-element.106.squares, s32[8,4,128]{2,1,0:T(4,128)S(1)} %get-tuple-element.107.meta, ...), custom_call_target="tpu_custom_call" | custom-call | tf_op jit(solution)/shard_map/cond/branch_2_fun/exchange312_352/pallas_call | solution.py:652
  107.6 12.1 %finish.1 = f32[3,8,512,128]{3,2,1,0:T(8,128)} custom-call(s32[8]{0:T(128)} %copy-done.5, s32[4096]{0:T(1024)S(1)} %bitcast.30, f32[8,128]{1,0:T(8,128)S(1)} %get-tuple-element.181.squares, f32[4,1560,128]{2,1,0:T(8,128)} %get-tuple-element.182.recv, f32[4,1536,128]{2,1,0:T(8,128)} %get-tuple-element.180.done), custom_call_target="tpu_custom_call" | custom-call | tf_op jit(solution)/shard_map/finish/pallas_call | solution.py:691
  (1 shorter events, 0.0 us)
Async XLA Ops:
  0.0 1.9 %copy-start = (f32[3,32,64,128]{3,2,1,0:T(8,128)S(1)}, f32[3,32,64,128]{3,2,1,0:T(8,128)}, u32[]{:S(2)}) copy-start(f32[3,32,64,128]{3,2,1,0:T(8,128)} %vel.3) | copy-start | bytes 9437188
  1.9 0.7 copy-start.3
  2.6 0.7 copy-start.4
  3.3 15.2 %copy-start.1 = (f32[3,32,64,128]{3,2,1,0:T(8,128)S(1)}, f32[3,32,64,128]{3,2,1,0:T(8,128)}, u32[]{:S(2)}) copy-start(f32[3,32,64,128]{3,2,1,0:T(8,128)} %vel.3) | copy-start | bytes 9437188
  17.8 0.6 copy-start.5
  18.5 0.9 copy-start.2

commit v6 on v5

--- a/solution.py
+++ b/solution.py
@@ -115,13 +115,15 @@
 
 
 def front_kernel(
-    sizes, tiers, capacity, region, direct, targets, lens, vel, plan, counts, halos, tier, order,
+    sizes, tiers, capacity, region, direct, targets, lens, vel, plan, counts, inside, halos, tier, order,
     z_faces, need, sums, near_part, far_part, send_sem, recv_sem, part_send, part_recv, own_sem,
 ):
     place = [lax.axis_index(axis) for axis in ("gx", "gy", "wa")]
     n_x, n_y, n_z = sizes
     comps, cells_x, cells_y, cells_z = vel.shape
     writers = n_x * n_y
+    load = pltpu.make_async_copy(vel, inside, own_sem.at[0])
+    load.start()
 
     def beside(axis, step):
         size = sizes[axis]
@@ -153,18 +155,19 @@
         for k, (src, dst, device) in enumerate(moves)
     ]
     c = place[2]
-    own = pltpu.make_async_copy(need, near_part.at[c], own_sem)
+    own = pltpu.make_async_copy(need, near_part.at[c], own_sem.at[1])
     own.start()
     first = [
         send_to(need, near_part.at[c], part_send.at[k], part_recv.at[k], device)
         for k, device in enumerate(mates)
     ]
+    load.wait()
     lane = lax.broadcasted_iota(jnp.int32, (cells_y, cells_z), 1)
 
     def plane(x, acc):
         here = lane == x
         rolled = [
-            pltpu.roll(vel[comp, x], lax.rem(x + last, cells_z), 1)
+            pltpu.roll(inside[comp, x], lax.rem(x + last, cells_z), 1)
             for last in range(2)
             for comp in (0, 1)
         ]
@@ -369,7 +372,7 @@
 
 def unpack(count, marks, source, target, lane, at):
     comps, width = lane.shape
-    group = math.gcd(marks[0].shape[-1], 32 if count <= 4 else 8)
+    group = math.gcd(marks[0].shape[-1], 32 if count <= 4 else 4)
     lists, k = marks
     per_line = lists.shape[2] // group
 
@@ -393,24 +396,38 @@
 
 
 def exchange_kernel(
-    n_x, n_y, n_z, comps, rows, direct, extra, send, squares, meta, spill, starts, recv, total, heard,
-    done, near_part, far_part, stage, marks, send_sem, recv_sem, part_send, part_recv, word_send,
-    word_recv, own_sem, done_sem, mark_sem, *rest,
+    n_x, n_y, n_z, comps, rows, direct, extra, send, squares, meta, spill, starts, total, heard, done,
+    near_part, far_part, stage, marks, send_sem, recv_sem, part_send, part_recv, word_send, word_recv,
+    own_sem, done_sem, mark_sem, *rest,
 ):
     c = lax.axis_index("wa")
     near, far = plane_order(n_x, n_y, 1)
     me = near[0][0] * n_y + near[0][1]
-    held, relay = rest[: len(near)], rest[len(near) :]
-    peers, mates = near[1:] + far, line_mates(n_z)
+    devices = near + far
+    held, relay = rest[: len(devices)], rest[len(devices) :]
+    half = halves(n_y)
+    inner = range(1, len(near))
+    outer = sorted(range(len(near), len(devices)), key=lambda k: ((k - len(near)) % half, k))
+    mates = line_mates(n_z)
     barrier = pltpu.get_barrier_semaphore()
-    for device in mates + peers:
+    for device in mates + devices[1:]:
         pl.semaphore_signal(barrier, inc=1, device_id=device, device_id_type=MESH)
-    pl.semaphore_wait(barrier, len(peers) + len(mates))
+    pl.semaphore_wait(barrier, len(devices) - 1 + len(mates))
 
     def number(device):
         return device[0] * n_y + device[1]
 
     whole = pl.ds(0, rows * comps)
+    short = pl.ds(0, direct * comps) if extra else whole
+    words, blocks, relays, copies = {}, {}, {}, []
+
+    def blocks_to(k):
+        used = whole if k < len(near) else short
+        blocks[k] = send_to(
+            send.at[number(devices[k]), used], held[k].at[used], send_sem.at[k], recv_sem.at[k],
+            devices[k],
+        )
+
     own = [
         pltpu.make_async_copy(squares, near_part.at[c], own_sem.at[0]),
         pltpu.make_async_copy(meta.at[me], marks.at[0], mark_sem.at[0]),
@@ -422,123 +439,104 @@
         send_to(squares, near_part.at[c], part_send.at[k], part_recv.at[k], device)
         for k, device in enumerate(mates)
     ]
-    relays, copies, words, blocks = [], [], [], []
     if extra:
         (
             landed, ready, begins, places, relay_send, relay_recv, spill_send, spill_recv, begin_sem
         ) = relay
         tiles = pl.ds(0, extra * comps // 8)
-        relays = [
+        poured = [
             send_to(starts, begins, spill_send.at[0], spill_recv.at[0], far[0]),
             send_to(spill.at[tiles], landed.at[tiles], spill_send.at[1], spill_recv.at[1], far[0]),
         ]
-    for k, device in enumerate(peers):
-        words.append(
-            send_to(meta.at[number(device)], heard.at[k + 1], word_send.at[k], word_recv.at[k], device)
+    for k in range(1, len(devices)):
+        words[k] = send_to(
+            meta.at[number(devices[k])], heard.at[k], word_send.at[k], word_recv.at[k], devices[k]
         )
-    short = pl.ds(0, direct * comps) if extra else whole
-    for k, device in enumerate(peers):
-        if k + 1 < len(near):
-            used, target = whole, held[k + 1].at[whole]
-        else:
-            used, target = short, recv.at[k + 1 - len(near), short]
-        blocks.append(
-            send_to(send.at[number(device), used], target, send_sem.at[k], recv_sem.at[k], device)
-        )
+    for k in inner:
+        blocks_to(k)
+    early = len(outer) // 2 if extra else len(outer)
+    for k in outer[:early]:
+        blocks_to(k)
     own[0].wait()
     for copy in first:
         copy.wait()
-    for k, device in enumerate(peers):
-        sem = n_z - 1 + k
+    for k in range(1, len(devices)):
+        sem = n_z - 2 + k
         copies.append(
-            send_to(near_part, far_part.at[k], part_send.at[sem], part_recv.at[sem], device)
+            send_to(near_part, far_part.at[k - 1], part_send.at[sem], part_recv.at[sem], devices[k])
         )
-    if extra:
-        relays[0].wait()
-        load = pltpu.make_async_copy(begins, places, begin_sem.at[0])
-        load.start()
-        load.wait()
-        relays[1].wait()
-        size = (rows - direct) * comps
-        half = halves(n_y)
-        for k, (x, y, _) in enumerate(near):
-            begin = places[0, x * half + lax.rem(y, half)] * comps
-
-            def tile(i, _, k=k, begin=begin):
-                ready[k, pl.ds(pl.multiple_of(i * 8, 8), 8), :] = landed[begin + i]
-                return 0
-
-            lax.fori_loop(0, size // 8, tile, 0)
-        past = pl.ds(direct * comps, size)
-        for k, device in enumerate(near):
-            if k:
-                copies.append(
-                    send_to(
-                        ready.at[k], recv.at[k, past], relay_send.at[k], relay_recv.at[k], device
-                    )
-                )
-        keep = pltpu.make_async_copy(ready.at[0], recv.at[0, past], begin_sem.at[1])
-        keep.start()
-        keep.wait()
     lane = lax.broadcasted_iota(jnp.int32, (comps, send.shape[2]), 1)
-    outs = []
-    for k in range(len(near)):
+
+    def place(k):
         if k:
-            words[k - 1].wait()
+            words[k].wait()
             load = pltpu.make_async_copy(heard.at[k], marks.at[k], mark_sem.at[k])
             load.start()
+            blocks[k].wait()
+            if k in relays:
+                relays[k].wait()
             load.wait()
-            blocks[k - 1].wait()
         else:
             own[1].wait()
             own[2].wait()
         unpack(len(near), (marks, k), held[k], stage, lane, k)
         out = pltpu.make_async_copy(stage.at[k], done.at[k], done_sem.at[k])
         out.start()
-        outs.append(out)
-    for copy in words[len(near) - 1 :] + blocks[len(near) - 1 :] + copies + outs:
+        copies.append(out)
+
+    place(0)
+    if extra:
+        poured[0].wait()
+        load = pltpu.make_async_copy(begins, places, begin_sem.at[0])
+        load.start()
+        load.wait()
+        poured[1].wait()
+        size = (rows - direct) * comps
+        for k, (x, y, _) in enumerate(near):
+            begin = places[0, x * half + lax.rem(y, half)] * comps
+
+            def tile(i, _, k=k, begin=begin):
+                ready[k, pl.ds(pl.multiple_of(i * 8, 8), 8), :] = landed[begin + i]
+                return 0
+
+            lax.fori_loop(0, size // 8, tile, 0)
+        past = pl.ds(direct * comps, size)
+        for k, device in enumerate(near):
+            target = held[len(near) + k].at[past]
+            if k:
+                relays[len(near) + k] = send_to(
+                    ready.at[k], target, relay_send.at[k], relay_recv.at[k], device
+                )
+            else:
+                def keep(i, _):
+                    at = pl.ds(pl.multiple_of(i * 8, 8), 8)
+                    held[len(near)][pl.ds(pl.multiple_of(direct * comps + i * 8, 8), 8), :] = ready[
+                        0, at, :
+                    ]
+                    return 0
+
+                lax.fori_loop(0, size // 8, keep, 0)
+    for k in outer[early:]:
+        blocks_to(k)
+    for k in inner:
+        place(k)
+    for k in outer:
+        place(k)
+    for copy in copies:
         copy.wait()
     total[...] = jnp.sum(near_part[...], axis=0) + jnp.sum(far_part[...], axis=(0, 1))
 
 
-def finish_kernel(every, near, order, meta, squares, recv, done, out, scale):
+def finish_kernel(every, order, squares, done, out, scale):
     comps, _, capacity, width = out.shape
-    step = pl.program_id(0)
-
-    @pl.when(step == 0)
+
+    @pl.when(pl.program_id(0) == 0)
     def _():
         total = jnp.sum(squares[...], keepdims=True)
         scale[...] = jnp.broadcast_to(1.0 / jnp.sqrt(total / every + 1e-06), scale.shape)
 
-    @pl.when(step < near)
-    def _():
-        for c in range(comps):
-            out[c, 0] = done[0, pl.ds(c, capacity, stride=comps), :] * scale[:1]
-
-    @pl.when(step >= near)
-    def _():
-        lane = lax.broadcasted_iota(jnp.int32, (comps, width), 1)
-        factor = scale[:comps]
-        group = math.gcd(capacity, 64)
-        first = step * capacity
-
-        def some(t, _):
-            start = first + t * group
-            for k in range(group):
-                mark = meta[start + k]
-                fields = jnp.full((comps, width), mark, jnp.int32)
-                ahead = lane + (lax.shift_right_logical(fields, 8) & 255)
-                row = lax.shift_right_logical(mark, 16)
-                head = recv[0, pl.ds(row, comps), :]
-                tail = recv[0, pl.ds(row + comps, comps), :]
-                joined = jnp.where(ahead >= width, head, tail)
-                moved = pltpu.roll(joined, lax.shift_right_logical(mark, 8) & (width - 1), 1)
-                value = jnp.where(lane < (fields & 255), moved * factor, 0.0)
-                for c in range(comps):
-                    out[c, 0, pl.ds(t * group + k, 1), :] = value[c : c + 1]
-            return 0
-
-        lax.fori_loop(0, capacity // group, some, 0)
+    for c in range(comps):
+        out[c, 0] = done[0, pl.ds(c, capacity, stride=comps), :] * scale[:1]
 
 
 def tier_sizes(capacity, n_y):
@@ -565,23 +563,23 @@
     direct, tiers = tier_sizes(capacity, n_y)
     most_extra = max([8] + [extra for _, extra in tiers])
     senders = n_x * halves(n_y)
-    beyond = max(1, writers - senders)
 
     smem = pl.BlockSpec(memory_space=pltpu.SMEM)
     vmem = pl.BlockSpec(memory_space=pltpu.VMEM)
     anywhere = pl.BlockSpec(memory_space=pl.ANY)
     dma = pltpu.SemaphoreType.DMA
-    plan, tallies, halos, tier, order = pl.pallas_call(
+    plan, tallies, inside, halos, tier, order = pl.pallas_call(
         functools.partial(front_kernel, (n_x, n_y, n_z), tiers, capacity, region, direct),
         out_shape=(
             jax.ShapeDtypeStruct((3, nblk // 128, 128), jnp.int32),
             jax.ShapeDtypeStruct((writers, 128), jnp.int32),
+            jax.ShapeDtypeStruct(velocity.shape, f32),
             jax.ShapeDtypeStruct((6, 2, max(cells_x, cells_y), cells_z), f32),
             jax.ShapeDtypeStruct((1,), jnp.int32),
             jax.ShapeDtypeStruct((writers,), jnp.int32),
         ),
-        in_specs=[vmem, vmem, vmem],
-        out_specs=(vmem, vmem, vmem, smem, smem),
+        in_specs=[vmem, vmem, anywhere],
+        out_specs=(vmem, vmem, vmem, vmem, smem, smem),
         scratch_shapes=[
             pltpu.VMEM((2, 2, cells_y, cells_z), f32),
             pltpu.VMEM((8, 128), f32),
@@ -592,10 +590,10 @@
             dma((8,)),
             dma((writers + n_z - 2,)),
             dma((writers + n_z - 2,)),
-            dma,
+            dma((2,)),
         ],
         compiler_params=pltpu.CompilerParams(
-            collective_id=1, has_side_effects=True, vmem_limit_bytes=16 * 2**20
+            collective_id=1, has_side_effects=True, vmem_limit_bytes=50 * 2**20
         ),
         name="front",
     )(destinations.reshape(nblk // 128, 128), lengths.reshape(nblk // 128, 128), velocity)
@@ -626,7 +624,7 @@
         plan.reshape(3 * nblk),
         tallies,
         jnp.zeros((writers * capacity,), jnp.int32),
-        velocity,
+        inside,
         halos,
         table,
     )
@@ -637,7 +635,7 @@
     def exchange(index, *operands):
         rows, extra = tiers[index]
         size = (rows - direct) * comps
-        held = [pltpu.VMEM(((rows + 8) * comps, width), f32) for _ in range(senders)]
+        held = [pltpu.VMEM(((rows + 8) * comps, width), f32) for _ in range(writers)]
         relay = [
             pltpu.VMEM(((extra * comps + size) // 8, 8, width), f32),
             pltpu.VMEM((senders, size, width), f32),
@@ -652,27 +650,26 @@
         return pl.pallas_call(
             functools.partial(exchange_kernel, n_x, n_y, n_z, comps, rows, direct, extra),
             out_shape=(
-                jax.ShapeDtypeStruct((beyond, region * comps, width), f32),
                 jax.ShapeDtypeStruct(squares.shape, f32),
                 jax.ShapeDtypeStruct(meta.shape, jnp.int32),
-                jax.ShapeDtypeStruct((senders, capacity * comps, width), f32),
+                jax.ShapeDtypeStruct((writers, capacity * comps, width), f32),
             ),
             in_specs=[anywhere, vmem, anywhere, anywhere, anywhere],
-            out_specs=(anywhere, vmem, anywhere, anywhere),
+            out_specs=(vmem, anywhere, anywhere),
             scratch_shapes=[
                 pltpu.VMEM((n_z,) + squares.shape, f32),
                 pltpu.VMEM((writers - 1, n_z) + squares.shape, f32),
-                pltpu.VMEM((senders, capacity * comps, width), f32),
-                pltpu.SMEM((senders,) + meta.shape[1:], jnp.int32),
-                dma((writers - 1,)),
-                dma((writers - 1,)),
+                pltpu.VMEM((writers, capacity * comps, width), f32),
+                pltpu.SMEM(meta.shape, jnp.int32),
+                dma((writers,)),
+                dma((writers,)),
                 dma((writers + n_z - 2,)),
                 dma((writers + n_z - 2,)),
-                dma((writers - 1,)),
-                dma((writers - 1,)),
+                dma((writers,)),
+                dma((writers,)),
                 dma((2,)),
-                dma((senders,)),
-                dma((senders,)),
+                dma((writers,)),
+                dma((writers,)),
             ]
             + held
             + (relay if extra else []),
@@ -683,27 +680,19 @@
         )(*operands)
 
     branches = [functools.partial(exchange, index) for index in range(len(tiers))]
-    arrived, squares, heard, done = lax.switch(
+    squares, heard, done = lax.switch(
         tier[0], branches, outgoing, squares, meta, spill, starts.reshape(1, 128)
     )
 
     every = velocity.size * n_x * n_y * n_z
     received = pl.pallas_call(
-        functools.partial(finish_kernel, float(every), senders),
+        functools.partial(finish_kernel, float(every)),
         grid_spec=pltpu.PrefetchScalarGridSpec(
             num_scalar_prefetch=1,
             grid=(writers,),
             in_specs=[
-                smem,
                 pl.BlockSpec((8, cells_z), lambda s, order: (0, 0)),
-                pl.BlockSpec(
-                    (1, region * comps, width),
-                    lambda s, order: (jnp.maximum(s - senders, 0), 0, 0),
-                ),
-                pl.BlockSpec(
-                    (1, capacity * comps, width),
-                    lambda s, order: (jnp.minimum(s, senders - 1), 0, 0),
-                ),
+                pl.BlockSpec((1, capacity * comps, width), lambda s, order: (s, 0, 0)),
             ],
             out_specs=pl.BlockSpec(
                 (comps, 1, capacity, width), lambda s, order: (0, order[s], 0, 0)
@@ -712,7 +701,7 @@
         ),
         out_shape=jax.ShapeDtypeStruct((comps, writers, capacity, width), f32),
         name="finish",
-    )(order, heard.reshape(writers * capacity), squares, arrived, done)
+    )(order, squares, done)
     return received.reshape(1, 1, comps, writers, capacity, width)
 
 

time: 118 us -> 118 us (level); the launches traced: 120 us -> 118 us
  local copies, waits for them, and re-layouts: 4.19 us -> 2.3 us
    pallas_call x1, Pallas kernels: 12.1 us -> 8.62 us  [local(): pl.pallas_call(functools.partial(finish_kernel, float(every)), grid_spec=...]
    pallas_call x1, Pallas kernels: 71.5 us -> 74.9 us  [exchange(): pl.pallas_call(functools.partial(exchange_kernel, n_x, n_y, n_z, comps, r...]
    unnamed x12 -> x8, local copies, waits for them, and re-layouts: 4.19 us -> 2.3 us
where the time goes in v6:
time: 118 us
  Pallas kernels  115 us (97%)
  local copies, waits for them, and re-layouts  2.3 us (2%)
    pallas_call x1, Pallas kernels, exchange(): pl.pallas_call(functools.partial(exchange_kernel, n_x, n_y, n_z, comps, r...  74.9 us
    pallas_call x1, Pallas kernels, local(): pl.pallas_call(functools.partial(blocks_kernel, n_x, n_y, region, direct)...  16.7 us
    pallas_call x1, Pallas kernels, local(): pl.pallas_call(functools.partial(front_kernel, (n_x, n_y, n_z), tiers, ca...  14.5 us
    pallas_call x1, Pallas kernels, local(): pl.pallas_call(functools.partial(finish_kernel, float(every)), grid_spec=...  8.62 us

profile of v6, /device:TPU:0, one launch (start us, length us, event | category | flops | bytes accessed | tf_op | source)
XLA Modules:
  0.0 118.0 jit_solution(6444482185699784749)
XLA Ops:
  0.0 0.0 copy-start.1
  0.0 0.7 copy-done.1
  0.7 0.0 copy-start.2
  0.7 0.7 copy-done.2
  1.4 14.5 %front.1 = (s32[3,16,128]{2,1,0:T(8,128)S(1)}, s32[8,128]{1,0:T(8,128)S(1)}, f32[3,32,64,128]{3,2,1,0:T(8,128)S(1)}, f32[6,2,64,128]{3,2,1,0:T(8,128)S(1)}, s32[1]{0:T(128)}, /*index=5*/s32[8]{0:T(128)S(1)}) custom-call(s32[16,128]{1,0:T(8,128)S(1)} %bitcast.9, s32[16,128]{1,0:T(8,128)S(1)} %bitcast.10, f32[3,32,64,128]{3,2,1,0:T(8,128)} %vel.1), custom_call_target="tpu_custom_call" | custom-call | tf_op jit(solution)/shard_map/front/pallas_call | solution.py:571
  15.9 0.0 copy-start.3
  16.6 0.0 copy-start
  16.6 0.9 copy-done
  17.5 16.7 %blocks.1 = (f32[12480,128]{1,0:T(8,128)S(1)}, f32[8,128]{1,0:T(8,128)S(1)}, s32[4096]{0:T(1024)S(1)}, f32[162,8,128]{2,1,0:T(8,128)S(1)}, s32[128]{0:T(128)S(1)}) custom-call(s32[6144]{0:T(1024)S(1)} %bitcast.8, s32[8,128]{1,0:T(8,128)S(1)} %get-tuple-element.123.tallies, s32[4096]{0:T(1024)S(1)} %broadcast_in_dim.3.blank, ...), custom_call_target="tpu_custom_call" | custom-call | tf_op jit(solution)/shard_map/blocks/pallas_call | solution.py:602
  34.2 0.0 copy-done.3
  34.2 75.1 %conditional.1 = (f32[8,128]{1,0:T(8,128)S(1)}, f32[8,1536,128]{2,1,0:T(8,128)}) conditional(s32[]{:T(128)} %bitcast.2, (f32[8,1560,128]{2,1,0:T(8,128)S(1)}, f32[8,128]{1,0:T(8,128)S(1)}, s32[8,4,128]{2,1,0:T(4,128)S(1)}, f32[162,8,128]{2,1,0:T(8,128)S(1)}, s32[1,128]{1,0:T(1,128)S(1)}) %tuple.48, ...), branch_computations={%region_0.0_spmd, %region_1.0_spmd, %region_2.0_spmd, %region_3.0_... | conditional | bytes 16 | solution.py:683
  34.2 74.9 %exchange312_288.1 = (f32[8,128]{1,0:T(8,128)S(1)}, s32[8,4,128]{2,1,0:T(4,128)}, f32[8,1536,128]{2,1,0:T(8,128)}) custom-call(f32[8,1560,128]{2,1,0:T(8,128)S(1)} %get-tuple-element.72.send, f32[8,128]{1,0:T(8,128)S(1)} %get-tuple-element.73.squares, s32[8,4,128]{2,1,0:T(4,128)S(1)} %get-tuple-element.74.meta, f32[162,8,128]{2,1,0:T(8,128)S(1)} %get-tuple-element.75.spill, ...), custom_call_target="tpu_custom_call" | custom-call | tf_op jit(solution)/shard_map/cond/branch_1_fun/exchange312_288/pallas_call | solution.py:650
  109.3 8.6 %finish.1 = f32[3,8,512,128]{3,2,1,0:T(8,128)} custom-call(s32[8]{0:T(128)} %copy-done.3, f32[8,128]{1,0:T(8,128)S(1)} %get-tuple-element.131.squares, f32[8,1536,128]{2,1,0:T(8,128)} %get-tuple-element.132.done), custom_call_target="tpu_custom_call" | custom-call | tf_op jit(solution)/shard_map/finish/pallas_call | solution.py:688
  (1 shorter events, 0.0 us)
Async XLA Ops:
  0.0 0.7 copy-start.1
  0.7 0.7 copy-start.2
  15.9 18.3 %copy-start.3 = (s32[8]{0:T(128)}, s32[8]{0:T(128)S(1)}, u32[]{:S(2)}) copy-start(s32[8]{0:T(128)S(1)} %get-tuple-element.120.order) | copy-start | bytes 100
  16.6 0.9 copy-start

commit v7 on v6

--- a/solution.py
+++ b/solution.py
@@ -115,7 +115,7 @@
 
 
 def front_kernel(
-    sizes, tiers, capacity, region, direct, targets, lens, vel, plan, counts, inside, halos, tier, order,
+    sizes, tiers, capacity, region, direct, targets, lens, vel, plan, counts, inside, halos, tier,
     z_faces, need, sums, near_part, far_part, send_sem, recv_sem, part_send, part_recv, own_sem,
 ):
     place = [lax.axis_index(axis) for axis in ("gx", "gy", "wa")]
@@ -178,9 +178,6 @@
     for last in range(2):
         for i in range(2):
             z_faces[last, i] = columns[2 * last + i]
-    near, far = plane_order(n_x, n_y, -1)
-    for k, (x, y, _) in enumerate(near + far):
-        order[k] = x * n_y + y
     own.wait()
     for copy in first:
         copy.wait()
@@ -372,7 +369,7 @@
 
 def unpack(count, marks, source, target, lane, at):
     comps, width = lane.shape
-    group = math.gcd(marks[0].shape[-1], 32 if count <= 4 else 4)
+    group = math.gcd(marks[0].shape[-1], 64 if count <= 4 else 4)
     lists, k = marks
     per_line = lists.shape[2] // group
 
@@ -404,6 +401,7 @@
     near, far = plane_order(n_x, n_y, 1)
     me = near[0][0] * n_y + near[0][1]
     devices = near + far
+    sources = sum(plane_order(n_x, n_y, -1), [])
     held, relay = rest[: len(devices)], rest[len(devices) :]
     half = halves(n_y)
     inner = range(1, len(near))
@@ -452,10 +450,7 @@
         words[k] = send_to(
             meta.at[number(devices[k])], heard.at[k], word_send.at[k], word_recv.at[k], devices[k]
         )
-    for k in inner:
-        blocks_to(k)
-    early = len(outer) // 2 if extra else len(outer)
-    for k in outer[:early]:
+    for k in list(inner) + list(outer):
         blocks_to(k)
     own[0].wait()
     for copy in first:
@@ -480,7 +475,8 @@
             own[1].wait()
             own[2].wait()
         unpack(len(near), (marks, k), held[k], stage, lane, k)
-        out = pltpu.make_async_copy(stage.at[k], done.at[k], done_sem.at[k])
+        spot = sources[k][0] * n_y + sources[k][1]
+        out = pltpu.make_async_copy(stage.at[k], done.at[spot], done_sem.at[k])
         out.start()
         copies.append(out)
 
@@ -516,8 +512,6 @@
                     return 0
 
                 lax.fori_loop(0, size // 8, keep, 0)
-    for k in outer[early:]:
-        blocks_to(k)
     for k in inner:
         place(k)
     for k in outer:
@@ -527,23 +521,24 @@
     total[...] = jnp.sum(near_part[...], axis=0) + jnp.sum(far_part[...], axis=(0, 1))
 
 
-def finish_kernel(every, order, squares, done, out, scale):
-    comps, _, capacity, width = out.shape
+def finish_kernel(every, squares, done, out, scale):
+    comps, together, capacity, width = out.shape
 
     @pl.when(pl.program_id(0) == 0)
     def _():
         total = jnp.sum(squares[...], keepdims=True)
         scale[...] = jnp.broadcast_to(1.0 / jnp.sqrt(total / every + 1e-06), scale.shape)
 
-    for c in range(comps):
-        out[c, 0] = done[0, pl.ds(c, capacity, stride=comps), :] * scale[:1]
+    for k in range(together):
+        for c in range(comps):
+            out[c, k] = done[k, pl.ds(c, capacity, stride=comps), :] * scale[:1]
 
 
 def tier_sizes(capacity, n_y):
     def up(part):
         return -(-capacity * part // (64 * 8)) * 8
 
-    direct = [(up(part), 0) for part in (52, 64)]
+    direct = [(up(part), 0) for part in (64,)]
     if n_y % 2:
         return up(64), direct
     parts = ((38, 28), (39, 36), (39, 44), (40, 54))
@@ -568,7 +563,7 @@
     vmem = pl.BlockSpec(memory_space=pltpu.VMEM)
     anywhere = pl.BlockSpec(memory_space=pl.ANY)
     dma = pltpu.SemaphoreType.DMA
-    plan, tallies, inside, halos, tier, order = pl.pallas_call(
+    plan, tallies, inside, halos, tier = pl.pallas_call(
         functools.partial(front_kernel, (n_x, n_y, n_z), tiers, capacity, region, direct),
         out_shape=(
             jax.ShapeDtypeStruct((3, nblk // 128, 128), jnp.int32),
@@ -576,10 +571,9 @@
             jax.ShapeDtypeStruct(velocity.shape, f32),
             jax.ShapeDtypeStruct((6, 2, max(cells_x, cells_y), cells_z), f32),
             jax.ShapeDtypeStruct((1,), jnp.int32),
-            jax.ShapeDtypeStruct((writers,), jnp.int32),
         ),
         in_specs=[vmem, vmem, anywhere],
-        out_specs=(vmem, vmem, vmem, vmem, smem, smem),
+        out_specs=(vmem, vmem, vmem, vmem, smem),
         scratch_shapes=[
             pltpu.VMEM((2, 2, cells_y, cells_z), f32),
             pltpu.VMEM((8, 128), f32),
@@ -685,23 +679,19 @@
     )
 
     every = velocity.size * n_x * n_y * n_z
+    together = math.gcd(writers, 2)
     received = pl.pallas_call(
         functools.partial(finish_kernel, float(every)),
-        grid_spec=pltpu.PrefetchScalarGridSpec(
-            num_scalar_prefetch=1,
-            grid=(writers,),
-            in_specs=[
-                pl.BlockSpec((8, cells_z), lambda s, order: (0, 0)),
-                pl.BlockSpec((1, capacity * comps, width), lambda s, order: (s, 0, 0)),
-            ],
-            out_specs=pl.BlockSpec(
-                (comps, 1, capacity, width), lambda s, order: (0, order[s], 0, 0)
-            ),
-            scratch_shapes=[pltpu.VMEM((8, width), f32)],
-        ),
+        grid=(writers // together,),
+        in_specs=[
+            pl.BlockSpec((8, cells_z), lambda s: (0, 0)),
+            pl.BlockSpec((together, capacity * comps, width), lambda s: (s, 0, 0)),
+        ],
+        out_specs=pl.BlockSpec((comps, together, capacity, width), lambda s: (0, s, 0, 0)),
+        scratch_shapes=[pltpu.VMEM((8, width), f32)],
         out_shape=jax.ShapeDtypeStruct((comps, writers, capacity, width), f32),
         name="finish",
-    )(order, squares, done)
+    )(squares, done)
     return received.reshape(1, 1, comps, writers, capacity, width)
 
 

time: 118 us -> 112 us (0.949)
  Pallas kernels: 115 us -> 108 us
    pallas_call x1, Pallas kernels: 74.9 us -> 71 us  [exchange(): pl.pallas_call(functools.partial(exchange_kernel, n_x, n_y, n_z, comps, r...]
    pallas_call x1, Pallas kernels: 8.62 us -> 6.04 us  [local(): pl.pallas_call(functools.partial(finish_kernel, float(every)), grid=(writ...]
where the time goes in v7:
time: 112 us
  Pallas kernels  108 us (96%)
  local copies, waits for them, and re-layouts  2.3 us (2%)
    pallas_call x1, Pallas kernels, exchange(): pl.pallas_call(functools.partial(exchange_kernel, n_x, n_y, n_z, comps, r...  71 us
    pallas_call x1, Pallas kernels, local(): pl.pallas_call(functools.partial(blocks_kernel, n_x, n_y, region, direct)...  17 us
    pallas_call x1, Pallas kernels, local(): pl.pallas_call(functools.partial(front_kernel, (n_x, n_y, n_z), tiers, ca...  14.5 us
    pallas_call x1, Pallas kernels, local(): pl.pallas_call(functools.partial(finish_kernel, float(every)), grid=(writ...  6.04 us
    unnamed x6, local copies, waits for them, and re-layouts  2.29 us

profile of v7, /device:TPU:0, one launch (start us, length us, event | category | flops | bytes accessed | tf_op | source)
XLA Modules:
  0.0 111.6 jit_solution(14683110411908567103)
XLA Ops:
  0.0 0.0 copy-start.1
  0.0 0.7 copy-done.1
  0.7 0.0 copy-start.2
  0.7 0.7 copy-done.2
  1.4 14.5 %front.1 = (s32[3,16,128]{2,1,0:T(8,128)S(1)}, s32[8,128]{1,0:T(8,128)S(1)}, f32[3,32,64,128]{3,2,1,0:T(8,128)S(1)}, f32[6,2,64,128]{3,2,1,0:T(8,128)S(1)}, s32[1]{0:T(128)}) custom-call(s32[16,128]{1,0:T(8,128)S(1)} %bitcast.9, s32[16,128]{1,0:T(8,128)S(1)} %bitcast.10, f32[3,32,64,128]{3,2,1,0:T(8,128)} %vel.1), custom_call_target="tpu_custom_call" | custom-call | tf_op jit(solution)/shard_map/front/pallas_call | solution.py:566
  16.5 0.0 copy-start
  16.5 0.9 copy-done
  17.4 17.0 %blocks.1 = (f32[12480,128]{1,0:T(8,128)S(1)}, f32[8,128]{1,0:T(8,128)S(1)}, s32[4096]{0:T(1024)S(1)}, f32[162,8,128]{2,1,0:T(8,128)S(1)}, s32[128]{0:T(128)S(1)}) custom-call(s32[6144]{0:T(1024)S(1)} %bitcast.8, s32[8,128]{1,0:T(8,128)S(1)} %get-tuple-element.104.tallies, s32[4096]{0:T(1024)S(1)} %broadcast_in_dim.3.blank, ...), custom_call_target="tpu_custom_call" | custom-call | tf_op jit(solution)/shard_map/blocks/pallas_call | solution.py:596
  34.4 71.2 %conditional.1 = (f32[8,128]{1,0:T(8,128)S(1)}, f32[8,1536,128]{2,1,0:T(8,128)}) conditional(s32[]{:T(128)} %bitcast.2, (f32[8,1560,128]{2,1,0:T(8,128)S(1)}, f32[8,128]{1,0:T(8,128)S(1)}, s32[8,4,128]{2,1,0:T(4,128)S(1)}, f32[162,8,128]{2,1,0:T(8,128)S(1)}, s32[1,128]{1,0:T(1,128)S(1)}) %tuple.41, ...), branch_computations={%region_0.0_spmd, %region_1.0_spmd, %region_2.0_spmd, %region_3.0_... | conditional | bytes 16 | solution.py:677
  34.4 71.0 %exchange312_288.1 = (f32[8,128]{1,0:T(8,128)S(1)}, s32[8,4,128]{2,1,0:T(4,128)}, f32[8,1536,128]{2,1,0:T(8,128)}) custom-call(f32[8,1560,128]{2,1,0:T(8,128)S(1)} %get-tuple-element.62.send, f32[8,128]{1,0:T(8,128)S(1)} %get-tuple-element.63.squares, s32[8,4,128]{2,1,0:T(4,128)S(1)} %get-tuple-element.64.meta, f32[162,8,128]{2,1,0:T(8,128)S(1)} %get-tuple-element.65.spill, ...), custom_call_target="tpu_custom_call" | custom-call | tf_op jit(solution)/shard_map/cond/branch_1_fun/exchange312_288/pallas_call | solution.py:644
  105.6 6.0 %finish.1 = f32[3,8,512,128]{3,2,1,0:T(8,128)} custom-call(f32[8,128]{1,0:T(8,128)S(1)} %get-tuple-element.112.squares, f32[8,1536,128]{2,1,0:T(8,128)} %get-tuple-element.113.done), custom_call_target="tpu_custom_call" | custom-call | tf_op jit(solution)/shard_map/finish/pallas_call | solution.py:683
  (1 shorter events, 0.0 us)
Async XLA Ops:
  0.0 0.7 copy-start.1
  0.7 0.7 copy-start.2
  16.5 0.9 copy-start
